TPU v7x, 8 devices: a whole 2x2x1 slice. The times are simulated.
8 devices in a mesh: row: 4 (over z, y, x), col: 2 (over core).
Axes of the slice: x: 2, y: 2, z: 1, core: 2. Of those that a mesh axis runs over, the one named last changes fastest.
Arguments:
- w_one: float32 [4, 2, 2, 768, 3072], P('row', 'col')
- w_two: float32 [4, 2, 2, 3072, 768], P('row', 'col')
- inputs: bfloat16 [4, 2, 3, 2048, 768], P('row', 'col')
- targets: bfloat16 [4, 2, 3, 2048, 768], P('row', 'col')
Outputs:
- output 1: float32 [4, 2, 2, 768, 3072], P('row', 'col')
- output 2: float32 [4, 2, 2, 3072, 768], P('row', 'col')
All inputs are finite; a program needn't handle non-finite values.
Results may differ from a plain program's by a relative error of at most 0.001.
Values are sent between devices in bfloat16 or wider.
A program may use at most 1 GiB of HBM per device.

v0:
```python
import jax
import jax.numpy as jnp
from jax import lax
from jax.sharding import PartitionSpec as P

LEARN_RATE = 1.5
NORM_EPS = 1e-6
GELU_C = 0.7978845608028654
GELU_K = 0.044715


def gelu_value(pre_act):
    tanh_inner = jnp.tanh(GELU_C * (pre_act + GELU_K * pre_act * pre_act * pre_act))
    return 0.5 * pre_act * (1.0 + tanh_inner)


def gelu_slope(pre_act):
    tanh_inner = jnp.tanh(GELU_C * (pre_act + GELU_K * pre_act * pre_act * pre_act))
    return 0.5 * (1.0 + tanh_inner) + 0.5 * pre_act * (1.0 - tanh_inner * tanh_inner) * GELU_C * (1.0 + 3.0 * GELU_K * pre_act * pre_act)


def local_grads(one_list, two_list, x_in, target):
    n_layers = len(one_list)
    one_lo = [w.astype(jnp.bfloat16) for w in one_list]
    two_lo = [w.astype(jnp.bfloat16) for w in two_list]
    hidden = x_in
    saved_acts = []
    for layer_idx in range(n_layers):
        hid_f = hidden.astype(jnp.float32)
        inv_rms = lax.rsqrt(jnp.mean(hid_f * hid_f, axis=-1, keepdims=True) + NORM_EPS)
        normed = hid_f * inv_rms
        normed_lo = normed.astype(jnp.bfloat16)
        pre_act = jnp.dot(normed_lo, one_lo[layer_idx], preferred_element_type=jnp.float32)
        act_lo = gelu_value(pre_act).astype(jnp.bfloat16)
        mlp_out = jnp.dot(act_lo, two_lo[layer_idx], preferred_element_type=jnp.float32)
        saved_acts.append((normed, inv_rms, normed_lo, pre_act, act_lo))
        hidden = (hid_f + mlp_out).astype(jnp.bfloat16)
    loss_scale = 2.0 / (x_in.shape[0] * x_in.shape[1])
    d_hidden = loss_scale * (hidden.astype(jnp.float32) - target.astype(jnp.float32))
    grads_one = [None] * n_layers
    grads_two = [None] * n_layers
    for layer_idx in reversed(range(n_layers)):
        normed, inv_rms, normed_lo, pre_act, act_lo = saved_acts[layer_idx]
        d_lo = d_hidden.astype(jnp.bfloat16)
        grads_two[layer_idx] = jnp.einsum('bf,bd->fd', act_lo, d_lo, preferred_element_type=jnp.float32)
        d_act = jnp.einsum('bd,fd->bf', d_lo, two_lo[layer_idx], preferred_element_type=jnp.float32)
        d_pre = (d_act * gelu_slope(pre_act)).astype(jnp.bfloat16)
        grads_one[layer_idx] = jnp.einsum('bd,bf->df', normed_lo, d_pre, preferred_element_type=jnp.float32)
        if layer_idx > 0:
            d_normed = jnp.einsum('bf,df->bd', d_pre, one_lo[layer_idx], preferred_element_type=jnp.float32)
            d_hidden = d_hidden + inv_rms * (d_normed - normed * jnp.mean(d_normed * normed, axis=-1, keepdims=True))
    return grads_one, grads_two


def solution(mesh):
    n_rows = mesh.shape['row']
    n_cols = mesh.shape['col']
    from_col_prev = [(i, (i + 1) % n_cols) for i in range(n_cols)]
    from_col_next = [(i, (i - 1) % n_cols) for i in range(n_cols)]
    from_row_prev = [(i, (i + 1) % n_rows) for i in range(n_rows)]
    from_row_next = [(i, (i - 1) % n_rows) for i in range(n_rows)]

    def device_fn(w_one, w_two, inputs, targets):
        n_layers = w_one.shape[2]
        one_list = [w_one[0, 0, k] for k in range(n_layers)]
        two_list = [w_two[0, 0, k] for k in range(n_layers)]
        for step_idx in range(inputs.shape[2]):
            grads_one, grads_two = local_grads(one_list, two_list, inputs[0, 0, step_idx], targets[0, 0, step_idx])
            upd_vals = [w - LEARN_RATE * g for w, g in zip(one_list + two_list, grads_one + grads_two)]
            wire_vals = [v.astype(jnp.bfloat16) for v in upd_vals]
            recv_cp = lax.ppermute(wire_vals, 'col', from_col_prev)
            recv_cn = lax.ppermute(wire_vals, 'col', from_col_next)
            recv_rp = lax.ppermute(wire_vals, 'row', from_row_prev)
            recv_rn = lax.ppermute(wire_vals, 'row', from_row_next)
            mixed_vals = [(own_val + cp_val.astype(jnp.float32) + cn_val.astype(jnp.float32) + rp_val.astype(jnp.float32) + rn_val.astype(jnp.float32)) / 5.0 for own_val, cp_val, cn_val, rp_val, rn_val in zip(upd_vals, recv_cp, recv_cn, recv_rp, recv_rn)]
            one_list = mixed_vals[:n_layers]
            two_list = mixed_vals[n_layers:]
        return jnp.stack(one_list)[None, None], jnp.stack(two_list)[None, None]

    grid_spec = P('row', 'col')
    return jax.shard_map(device_fn, mesh=mesh, in_specs=(grid_spec, grid_spec, grid_spec, grid_spec), out_specs=(grid_spec, grid_spec), check_vma=False)
```

profile of v0, /device:TPU:0, one launch (start us, length us, event | category | flops | bytes accessed | tf_op | source)
XLA Modules:
  0.0 2934.5 jit_solution(14563304763255573385)
XLA Ops:
  57.3 29.1 fusion.154
  104.9 32.6 %fusion.8 = bf16[2048,3072]{1,0:T(8,128)(2,1)} fusion(f32[2048,3072]{1,0:T(8,128)} %fusion.154, f32[1,1,2,3072,768]{4,3,2,1,0:T(8,128)} %param.5, bf16[2048,768]{0,1:T(8,128)(2,1)S(1)} %fusion.114, bf16[1,1,1,2048,768]{3,4,2,1,0:T(8,128)(2,1)S(1)} %copy-done.9), kind=kOutput, calls=%fused_computation.20 | convolution fusion | flops 9791078400 | bytes 48758784 | tf_op jit(solution)/shard_map/bd,fd->bf/dot_general | solution.py:46
  159.4 39.4 %fusion.206 = (bf16[768,3072]{1,0:T(8,128)(2,1)}, f32[768,3072]{1,0:T(8,128)}) fusion(f32[2048,3072]{1,0:T(8,128)} %fusion.132, bf16[2048,768]{0,1:T(8,128)(2,1)} %fusion.112, f32[1,1,2,3072,768]{4,3,2,1,0:T(8,128)} %param.5, bf16[1,1,1,2048,768]{3,4,2,1,0:T(8,128)(2,1)S(1)} %copy-done.5, f32[2048]{0:T(1024)S(1)} %copy-done.22, ...), kind=kOutput, calls=%fused_computation.260 | convolution fusion | flops 19458686976 | bytes 59777024 | tf_op jit(solution)/shard_map/bd,bf->df/dot_general | solution.py:48
  203.1 24.8 fusion.205
  271.1 26.6 fusion.207
  305.3 102.1 %collective-permute-done.1 = bf16[768,3072]{1,0:T(8,128)(2,1)} collective-permute-done((bf16[768,3072]{1,0:T(8,128)(2,1)}, bf16[768,3072]{1,0:T(8,128)(2,1)}, u32[]{:S(2)}, u32[]{:S(2)}) %collective-permute-start.1) | collective-permute-done | bytes 4718624 | tf_op jit(solution)/shard_map/ppermute | solution.py:73
  408.9 22.9 fusion.136
  431.8 75.7 %collective-permute-done.5 = bf16[3072,768]{1,0:T(8,128)(2,1)} collective-permute-done((bf16[3072,768]{1,0:T(8,128)(2,1)}, bf16[3072,768]{1,0:T(8,128)(2,1)}, u32[]{:S(2)}, u32[]{:S(2)}) %collective-permute-start.5) | collective-permute-done | bytes 4718624 | tf_op jit(solution)/shard_map/ppermute | solution.py:74
  509.9 99.7 %collective-permute-done.4 = bf16[3072,768]{1,0:T(8,128)(2,1)} collective-permute-done((bf16[3072,768]{1,0:T(8,128)(2,1)}, bf16[3072,768]{1,0:T(8,128)(2,1)}, u32[]{:S(2)}, u32[]{:S(2)}) %collective-permute-start.4) | collective-permute-done | bytes 4718624 | tf_op jit(solution)/shard_map/ppermute | solution.py:73
  624.5 186.3 %collective-permute-done.8 = bf16[768,3072]{1,0:T(8,128)(2,1)} collective-permute-done((bf16[768,3072]{1,0:T(8,128)(2,1)}, bf16[768,3072]{1,0:T(8,128)(2,1)}, u32[]{:S(2)}, u32[]{:S(2)}) %collective-permute-start.8) | collective-permute-done | bytes 4718624 | tf_op jit(solution)/shard_map/ppermute | solution.py:74
  829.2 184.0 %collective-permute-done.7 = bf16[768,3072]{1,0:T(8,128)(2,1)} collective-permute-done((bf16[768,3072]{1,0:T(8,128)(2,1)}, bf16[768,3072]{1,0:T(8,128)(2,1)}, u32[]{:S(2)}, u32[]{:S(2)}) %collective-permute-start.7) | collective-permute-done | bytes 4718624 | tf_op jit(solution)/shard_map/ppermute | solution.py:73
  1070.2 31.3 %fusion.22 = bf16[2048,3072]{1,0:T(8,128)(2,1)} fusion(f32[2048,3072]{1,0:T(8,128)} %fusion.151, f32[3072,768]{1,0:T(8,128)} %fusion.53, bf16[2048,768]{0,1:T(8,128)(2,1)} %fusion.116, bf16[1,1,1,2048,768]{3,4,2,1,0:T(8,128)(2,1)S(1)} %copy-done.7), kind=kOutput, calls=%fused_computation.34 | convolution fusion | flops 9793437696 | bytes 53477376 | tf_op jit(solution)/shard_map/bd,fd->bf/dot_general | solution.py:46
  1122.6 24.8 fusion.209
  1147.3 40.1 %fusion.210 = (bf16[768,3072]{1,0:T(8,128)(2,1)}, f32[768,3072]{1,0:T(8,128)}) fusion(f32[2048,3072]{1,0:T(8,128)} %fusion.136, bf16[2048,768]{0,1:T(8,128)(2,1)} %fusion.107, f32[3072,768]{1,0:T(8,128)} %fusion.47, bf16[1,1,1,2048,768]{3,4,2,1,0:T(8,128)(2,1)S(1)} %copy-done.4, f32[2048]{0:T(1024)S(1)} %copy-done.20, ...), kind=kOutput, calls=%fused_computation.264 | convolution fusion | flops 19479920640 | bytes 78651392 | tf_op jit(solution)/shard_map/bd,bf->df/dot_general | solution.py:48
  1211.3 25.5 fusion.213
  1236.8 55.4 %collective-permute-done.14 = bf16[768,3072]{1,0:T(8,128)(2,1)} collective-permute-done((bf16[768,3072]{1,0:T(8,128)(2,1)}, bf16[768,3072]{1,0:T(8,128)(2,1)}, u32[]{:S(2)}, u32[]{:S(2)}) %collective-permute-start.14) | collective-permute-done | bytes 4718624 | tf_op jit(solution)/shard_map/ppermute | solution.py:74
  1292.1 100.8 %collective-permute-done.13 = bf16[768,3072]{1,0:T(8,128)(2,1)} collective-permute-done((bf16[768,3072]{1,0:T(8,128)(2,1)}, bf16[768,3072]{1,0:T(8,128)(2,1)}, u32[]{:S(2)}, u32[]{:S(2)}) %collective-permute-start.13) | collective-permute-done | bytes 4718624 | tf_op jit(solution)/shard_map/ppermute | solution.py:73
  1419.1 75.3 %collective-permute-done.17 = bf16[3072,768]{1,0:T(8,128)(2,1)} collective-permute-done((bf16[3072,768]{1,0:T(8,128)(2,1)}, bf16[3072,768]{1,0:T(8,128)(2,1)}, u32[]{:S(2)}, u32[]{:S(2)}) %collective-permute-start.17) | collective-permute-done | bytes 4718624 | tf_op jit(solution)/shard_map/ppermute | solution.py:74
  1496.6 98.6 %collective-permute-done.16 = bf16[3072,768]{1,0:T(8,128)(2,1)} collective-permute-done((bf16[3072,768]{1,0:T(8,128)(2,1)}, bf16[3072,768]{1,0:T(8,128)(2,1)}, u32[]{:S(2)}, u32[]{:S(2)}) %collective-permute-start.16) | collective-permute-done | bytes 4718624 | tf_op jit(solution)/shard_map/ppermute | solution.py:73
  1605.8 191.9 %collective-permute-done.20 = bf16[768,3072]{1,0:T(8,128)(2,1)} collective-permute-done((bf16[768,3072]{1,0:T(8,128)(2,1)}, bf16[768,3072]{1,0:T(8,128)(2,1)}, u32[]{:S(2)}, u32[]{:S(2)}) %collective-permute-start.20) | collective-permute-done | bytes 4718624 | tf_op jit(solution)/shard_map/ppermute | solution.py:74
  1813.3 184.8 %collective-permute-done.19 = bf16[768,3072]{1,0:T(8,128)(2,1)} collective-permute-done((bf16[768,3072]{1,0:T(8,128)(2,1)}, bf16[768,3072]{1,0:T(8,128)(2,1)}, u32[]{:S(2)}, u32[]{:S(2)}) %collective-permute-start.19) | collective-permute-done | bytes 4718624 | tf_op jit(solution)/shard_map/ppermute | solution.py:73
  2052.0 31.6 %fusion.36 = bf16[2048,3072]{1,0:T(8,128)(2,1)} fusion(f32[2048,3072]{1,0:T(8,128)} %fusion.148, f32[3072,768]{1,0:T(8,128)} %fusion.65, bf16[2048,768]{0,1:T(8,128)(2,1)} %fusion.118, bf16[1,1,1,2048,768]{3,4,2,1,0:T(8,128)(2,1)S(1)} %copy-done.6), kind=kOutput, calls=%fused_computation.48 | convolution fusion | flops 9793437696 | bytes 53477376 | tf_op jit(solution)/shard_map/bd,fd->bf/dot_general | solution.py:46
  2083.6 25.2 fusion.218
  2132.9 39.5 %fusion.215 = (bf16[768,3072]{1,0:T(8,128)(2,1)}, f32[768,3072]{1,0:T(8,128)}) fusion(f32[2048,3072]{1,0:T(8,128)} %fusion.134, bf16[2048,768]{0,1:T(8,128)(2,1)} %fusion.102, f32[3072,768]{1,0:T(8,128)} %copy-done.11, bf16[1,1,1,2048,768]{3,4,2,1,0:T(8,128)(2,1)S(1)} %copy-done.2, f32[2048]{0:T(1024)S(1)} %copy-done.18, ...), kind=kOutput, calls=%fused_computation.267 | convolution fusion | flops 19479920640 | bytes 78651392 | tf_op jit(solution)/shard_map/bd,bf->df/dot_general | solution.py:48
  2175.3 24.8 fusion.219
  2215.6 99.9 %collective-permute-done.34 = bf16[3072,768]{1,0:T(8,128)(2,1)} collective-permute-done((bf16[3072,768]{1,0:T(8,128)(2,1)}, bf16[3072,768]{1,0:T(8,128)(2,1)}, u32[]{:S(2)}, u32[]{:S(2)}) %collective-permute-start.34) | collective-permute-done | bytes 4718624 | tf_op jit(solution)/shard_map/ppermute | solution.py:73
  2316.8 99.0 %collective-permute-done.26 = bf16[768,3072]{1,0:T(8,128)(2,1)} collective-permute-done((bf16[768,3072]{1,0:T(8,128)(2,1)}, bf16[768,3072]{1,0:T(8,128)(2,1)}, u32[]{:S(2)}, u32[]{:S(2)}) %collective-permute-start.26) | collective-permute-done | bytes 4718624 | tf_op jit(solution)/shard_map/ppermute | solution.py:74
  2432.7 84.1 %collective-permute-done.32 = bf16[3072,768]{1,0:T(8,128)(2,1)} collective-permute-done((bf16[3072,768]{1,0:T(8,128)(2,1)}, bf16[3072,768]{1,0:T(8,128)(2,1)}, u32[]{:S(2)}, u32[]{:S(2)}) %collective-permute-start.32) | collective-permute-done | bytes 4718624 | tf_op jit(solution)/shard_map/ppermute | solution.py:74
  2519.9 98.9 %collective-permute-done.31 = bf16[3072,768]{1,0:T(8,128)(2,1)} collective-permute-done((bf16[3072,768]{1,0:T(8,128)(2,1)}, bf16[3072,768]{1,0:T(8,128)(2,1)}, u32[]{:S(2)}, u32[]{:S(2)}) %collective-permute-start.31) | collective-permute-done | bytes 4718624 | tf_op jit(solution)/shard_map/ppermute | solution.py:73
  2645.3 74.7 %collective-permute-done.25 = bf16[768,3072]{1,0:T(8,128)(2,1)} collective-permute-done((bf16[768,3072]{1,0:T(8,128)(2,1)}, bf16[768,3072]{1,0:T(8,128)(2,1)}, u32[]{:S(2)}, u32[]{:S(2)}) %collective-permute-start.25) | collective-permute-done | bytes 4718624 | tf_op jit(solution)/shard_map/ppermute | solution.py:73
  2726.8 93.4 %collective-permute-done.29 = bf16[768,3072]{1,0:T(8,128)(2,1)S(1)} collective-permute-done((bf16[768,3072]{1,0:T(8,128)(2,1)}, bf16[768,3072]{1,0:T(8,128)(2,1)S(1)}, u32[]{:S(2)}, u32[]{:S(2)}) %collective-permute-start.29) | collective-permute-done | bytes 4718624 | tf_op jit(solution)/shard_map/ppermute | solution.py:74
  2820.2 99.1 %collective-permute-done.28 = bf16[768,3072]{1,0:T(8,128)(2,1)} collective-permute-done((bf16[768,3072]{1,0:T(8,128)(2,1)}, bf16[768,3072]{1,0:T(8,128)(2,1)}, u32[]{:S(2)}, u32[]{:S(2)}) %collective-permute-start.28) | collective-permute-done | bytes 4718624 | tf_op jit(solution)/shard_map/ppermute | solution.py:73
  (179 shorter events, 511.1 us)
Async XLA Ops:
  203.1 204.3 %collective-permute-start.1 = (bf16[768,3072]{1,0:T(8,128)(2,1)}, bf16[768,3072]{1,0:T(8,128)(2,1)}, u32[]{:S(2)}, u32[]{:S(2)}) collective-permute-start(bf16[768,3072]{1,0:T(8,128)(2,1)} %get-tuple-element.16), channel_id=1, source_target_pairs={{0,2},{2,4},{4,6},{6,0},{1,3},{3,5},{5,7},{7,1}} | collective-permute-start | bytes 14155784 | tf_op jit(solution)/shard_map/ppermute | solution.py:73
  203.1 205.7 %collective-permute-start = (bf16[768,3072]{1,0:T(8,128)(2,1)}, bf16[768,3072]{1,0:T(8,128)(2,1)}, u32[]{:S(2)}, u32[]{:S(2)}) collective-permute-start(bf16[768,3072]{1,0:T(8,128)(2,1)} %get-tuple-element.16), channel_id=1, source_target_pairs={{0,1},{1,0},{2,3},{3,2},{4,5},{5,4},{6,7},{7,6}} | collective-permute-start | bytes 14155784 | tf_op jit(solution)/shard_map/ppermute | solution.py:71
  227.9 279.6 %collective-permute-start.5 = (bf16[3072,768]{1,0:T(8,128)(2,1)}, bf16[3072,768]{1,0:T(8,128)(2,1)}, u32[]{:S(2)}, u32[]{:S(2)}) collective-permute-start(bf16[3072,768]{1,0:T(8,128)(2,1)} %get-tuple-element.14), channel_id=1, source_target_pairs={{0,6},{2,0},{4,2},{6,4},{1,7},{3,1},{5,3},{7,5}} | collective-permute-start | bytes 14155784 | tf_op jit(solution)/shard_map/ppermute | solution.py:74
  230.8 378.8 %collective-permute-start.4 = (bf16[3072,768]{1,0:T(8,128)(2,1)}, bf16[3072,768]{1,0:T(8,128)(2,1)}, u32[]{:S(2)}, u32[]{:S(2)}) collective-permute-start(bf16[3072,768]{1,0:T(8,128)(2,1)} %get-tuple-element.14), channel_id=1, source_target_pairs={{0,2},{2,4},{4,6},{6,0},{1,3},{3,5},{5,7},{7,1}} | collective-permute-start | bytes 14155784 | tf_op jit(solution)/shard_map/ppermute | solution.py:73
  305.3 305.9 %collective-permute-start.3 = (bf16[3072,768]{1,0:T(8,128)(2,1)}, bf16[3072,768]{1,0:T(8,128)(2,1)}, u32[]{:S(2)}, u32[]{:S(2)}) collective-permute-start(bf16[3072,768]{1,0:T(8,128)(2,1)} %get-tuple-element.14), channel_id=1, source_target_pairs={{0,1},{1,0},{2,3},{3,2},{4,5},{5,4},{6,7},{7,6}} | collective-permute-start | bytes 14155784 | tf_op jit(solution)/shard_map/ppermute | solution.py:71
  407.4 634.3 %collective-permute-start.11 = (bf16[3072,768]{1,0:T(8,128)(2,1)}, bf16[3072,768]{1,0:T(8,128)(2,1)}, u32[]{:S(2)}, u32[]{:S(2)}) collective-permute-start(bf16[3072,768]{1,0:T(8,128)(2,1)} %get-tuple-element.20), channel_id=1, source_target_pairs={{0,6},{2,0},{4,2},{6,4},{1,7},{3,1},{5,3},{7,5}} | collective-permute-start | bytes 14155784 | tf_op jit(solution)/shard_map/ppermute | solution.py:74
  408.8 402.0 %collective-permute-start.8 = (bf16[768,3072]{1,0:T(8,128)(2,1)}, bf16[768,3072]{1,0:T(8,128)(2,1)}, u32[]{:S(2)}, u32[]{:S(2)}) collective-permute-start(bf16[768,3072]{1,0:T(8,128)(2,1)} %get-tuple-element.10), channel_id=1, source_target_pairs={{0,6},{2,0},{4,2},{6,4},{1,7},{3,1},{5,3},{7,5}} | collective-permute-start | bytes 14155784 | tf_op jit(solution)/shard_map/ppermute | solution.py:74
  507.5 534.2 %collective-permute-start.10 = (bf16[3072,768]{1,0:T(8,128)(2,1)}, bf16[3072,768]{1,0:T(8,128)(2,1)}, u32[]{:S(2)}, u32[]{:S(2)}) collective-permute-start(bf16[3072,768]{1,0:T(8,128)(2,1)} %get-tuple-element.20), channel_id=1, source_target_pairs={{0,2},{2,4},{4,6},{6,0},{1,3},{3,5},{5,7},{7,1}} | collective-permute-start | bytes 14155784 | tf_op jit(solution)/shard_map/ppermute | solution.py:73
  609.6 403.6 %collective-permute-start.7 = (bf16[768,3072]{1,0:T(8,128)(2,1)}, bf16[768,3072]{1,0:T(8,128)(2,1)}, u32[]{:S(2)}, u32[]{:S(2)}) collective-permute-start(bf16[768,3072]{1,0:T(8,128)(2,1)} %get-tuple-element.10), channel_id=1, source_target_pairs={{0,2},{2,4},{4,6},{6,0},{1,3},{3,5},{5,7},{7,1}} | collective-permute-start | bytes 14155784 | tf_op jit(solution)/shard_map/ppermute | solution.py:73
  611.1 402.1 %collective-permute-start.6 = (bf16[768,3072]{1,0:T(8,128)(2,1)}, bf16[768,3072]{1,0:T(8,128)(2,1)}, u32[]{:S(2)}, u32[]{:S(2)}) collective-permute-start(bf16[768,3072]{1,0:T(8,128)(2,1)} %get-tuple-element.10), channel_id=1, source_target_pairs={{0,1},{1,0},{2,3},{3,2},{4,5},{5,4},{6,7},{7,6}} | collective-permute-start | bytes 14155784 | tf_op jit(solution)/shard_map/ppermute | solution.py:71
  810.9 230.9 %collective-permute-start.9 = (bf16[3072,768]{1,0:T(8,128)(2,1)}, bf16[3072,768]{1,0:T(8,128)(2,1)}, u32[]{:S(2)}, u32[]{:S(2)}) collective-permute-start(bf16[3072,768]{1,0:T(8,128)(2,1)} %get-tuple-element.20), channel_id=1, source_target_pairs={{0,1},{1,0},{2,3},{3,2},{4,5},{5,4},{6,7},{7,6}} | collective-permute-start | bytes 14155784 | tf_op jit(solution)/shard_map/ppermute | solution.py:71
  1189.5 205.9 %collective-permute-start.12 = (bf16[768,3072]{1,0:T(8,128)(2,1)}, bf16[768,3072]{1,0:T(8,128)(2,1)}, u32[]{:S(2)}, u32[]{:S(2)}) collective-permute-start(bf16[768,3072]{1,0:T(8,128)(2,1)} %get-tuple-element.28), channel_id=1, source_target_pairs={{0,1},{1,0},{2,3},{3,2},{4,5},{5,4},{6,7},{7,6}} | collective-permute-start | bytes 14155784 | tf_op jit(solution)/shard_map/ppermute | solution.py:71
  1209.1 285.3 %collective-permute-start.17 = (bf16[3072,768]{1,0:T(8,128)(2,1)}, bf16[3072,768]{1,0:T(8,128)(2,1)}, u32[]{:S(2)}, u32[]{:S(2)}) collective-permute-start(bf16[3072,768]{1,0:T(8,128)(2,1)} %get-tuple-element.26), channel_id=1, source_target_pairs={{0,6},{2,0},{4,2},{6,4},{1,7},{3,1},{5,3},{7,5}} | collective-permute-start | bytes 14155784 | tf_op jit(solution)/shard_map/ppermute | solution.py:74
  1211.2 384.0 %collective-permute-start.16 = (bf16[3072,768]{1,0:T(8,128)(2,1)}, bf16[3072,768]{1,0:T(8,128)(2,1)}, u32[]{:S(2)}, u32[]{:S(2)}) collective-permute-start(bf16[3072,768]{1,0:T(8,128)(2,1)} %get-tuple-element.26), channel_id=1, source_target_pairs={{0,2},{2,4},{4,6},{6,0},{1,3},{3,5},{5,7},{7,1}} | collective-permute-start | bytes 14155784 | tf_op jit(solution)/shard_map/ppermute | solution.py:73
  1292.1 304.6 %collective-permute-start.15 = (bf16[3072,768]{1,0:T(8,128)(2,1)}, bf16[3072,768]{1,0:T(8,128)(2,1)}, u32[]{:S(2)}, u32[]{:S(2)}) collective-permute-start(bf16[3072,768]{1,0:T(8,128)(2,1)} %get-tuple-element.26), channel_id=1, source_target_pairs={{0,1},{1,0},{2,3},{3,2},{4,5},{5,4},{6,7},{7,6}} | collective-permute-start | bytes 14155784 | tf_op jit(solution)/shard_map/ppermute | solution.py:71
  1393.0 628.2 %collective-permute-start.23 = (bf16[3072,768]{1,0:T(8,128)(2,1)}, bf16[3072,768]{1,0:T(8,128)(2,1)}, u32[]{:S(2)}, u32[]{:S(2)}) collective-permute-start(bf16[3072,768]{1,0:T(8,128)(2,1)} %get-tuple-element.32), channel_id=1, source_target_pairs={{0,6},{2,0},{4,2},{6,4},{1,7},{3,1},{5,3},{7,5}} | collective-permute-start | bytes 14155784 | tf_op jit(solution)/shard_map/ppermute | solution.py:74
  1395.4 402.3 %collective-permute-start.20 = (bf16[768,3072]{1,0:T(8,128)(2,1)}, bf16[768,3072]{1,0:T(8,128)(2,1)}, u32[]{:S(2)}, u32[]{:S(2)}) collective-permute-start(bf16[768,3072]{1,0:T(8,128)(2,1)} %get-tuple-element.22), channel_id=1, source_target_pairs={{0,6},{2,0},{4,2},{6,4},{1,7},{3,1},{5,3},{7,5}} | collective-permute-start | bytes 14155784 | tf_op jit(solution)/shard_map/ppermute | solution.py:74
  1494.4 526.8 %collective-permute-start.22 = (bf16[3072,768]{1,0:T(8,128)(2,1)}, bf16[3072,768]{1,0:T(8,128)(2,1)}, u32[]{:S(2)}, u32[]{:S(2)}) collective-permute-start(bf16[3072,768]{1,0:T(8,128)(2,1)} %get-tuple-element.32), channel_id=1, source_target_pairs={{0,2},{2,4},{4,6},{6,0},{1,3},{3,5},{5,7},{7,1}} | collective-permute-start | bytes 14155784 | tf_op jit(solution)/shard_map/ppermute | solution.py:73
  1595.2 402.9 %collective-permute-start.19 = (bf16[768,3072]{1,0:T(8,128)(2,1)}, bf16[768,3072]{1,0:T(8,128)(2,1)}, u32[]{:S(2)}, u32[]{:S(2)}) collective-permute-start(bf16[768,3072]{1,0:T(8,128)(2,1)} %get-tuple-element.22), channel_id=1, source_target_pairs={{0,2},{2,4},{4,6},{6,0},{1,3},{3,5},{5,7},{7,1}} | collective-permute-start | bytes 14155784 | tf_op jit(solution)/shard_map/ppermute | solution.py:73
  1596.7 401.4 %collective-permute-start.18 = (bf16[768,3072]{1,0:T(8,128)(2,1)}, bf16[768,3072]{1,0:T(8,128)(2,1)}, u32[]{:S(2)}, u32[]{:S(2)}) collective-permute-start(bf16[768,3072]{1,0:T(8,128)(2,1)} %get-tuple-element.22), channel_id=1, source_target_pairs={{0,1},{1,0},{2,3},{3,2},{4,5},{5,4},{6,7},{7,6}} | collective-permute-start | bytes 14155784 | tf_op jit(solution)/shard_map/ppermute | solution.py:71
  1797.7 223.4 %collective-permute-start.21 = (bf16[3072,768]{1,0:T(8,128)(2,1)}, bf16[3072,768]{1,0:T(8,128)(2,1)}, u32[]{:S(2)}, u32[]{:S(2)}) collective-permute-start(bf16[3072,768]{1,0:T(8,128)(2,1)} %get-tuple-element.32), channel_id=1, source_target_pairs={{0,1},{1,0},{2,3},{3,2},{4,5},{5,4},{6,7},{7,6}} | collective-permute-start | bytes 14155784 | tf_op jit(solution)/shard_map/ppermute | solution.py:71
  2111.0 204.5 %collective-permute-start.34 = (bf16[3072,768]{1,0:T(8,128)(2,1)}, bf16[3072,768]{1,0:T(8,128)(2,1)}, u32[]{:S(2)}, u32[]{:S(2)}) collective-permute-start(bf16[3072,768]{1,0:T(8,128)(2,1)} %get-tuple-element.40), channel_id=1, source_target_pairs={{0,2},{2,4},{4,6},{6,0},{1,3},{3,5},{5,7},{7,1}} | collective-permute-start | bytes 14155784 | tf_op jit(solution)/shard_map/ppermute | solution.py:73
  2111.0 204.5 %collective-permute-start.33 = (bf16[3072,768]{1,0:T(8,128)(2,1)}, bf16[3072,768]{1,0:T(8,128)(2,1)}, u32[]{:S(2)}, u32[]{:S(2)}) collective-permute-start(bf16[3072,768]{1,0:T(8,128)(2,1)} %get-tuple-element.40), channel_id=1, source_target_pairs={{0,1},{1,0},{2,3},{3,2},{4,5},{5,4},{6,7},{7,6}} | collective-permute-start | bytes 14155784 | tf_op jit(solution)/shard_map/ppermute | solution.py:71
  2172.4 243.3 %collective-permute-start.26 = (bf16[768,3072]{1,0:T(8,128)(2,1)}, bf16[768,3072]{1,0:T(8,128)(2,1)}, u32[]{:S(2)}, u32[]{:S(2)}) collective-permute-start(bf16[768,3072]{1,0:T(8,128)(2,1)} %get-tuple-element.38), channel_id=1, source_target_pairs={{0,6},{2,0},{4,2},{6,4},{1,7},{3,1},{5,3},{7,5}} | collective-permute-start | bytes 14155784 | tf_op jit(solution)/shard_map/ppermute | solution.py:74
  2200.2 316.7 %collective-permute-start.32 = (bf16[3072,768]{1,0:T(8,128)(2,1)}, bf16[3072,768]{1,0:T(8,128)(2,1)}, u32[]{:S(2)}, u32[]{:S(2)}) collective-permute-start(bf16[3072,768]{1,0:T(8,128)(2,1)} %get-tuple-element.42), channel_id=1, source_target_pairs={{0,6},{2,0},{4,2},{6,4},{1,7},{3,1},{5,3},{7,5}} | collective-permute-start | bytes 14155784 | tf_op jit(solution)/shard_map/ppermute | solution.py:74
  2213.5 405.3 %collective-permute-start.31 = (bf16[3072,768]{1,0:T(8,128)(2,1)}, bf16[3072,768]{1,0:T(8,128)(2,1)}, u32[]{:S(2)}, u32[]{:S(2)}) collective-permute-start(bf16[3072,768]{1,0:T(8,128)(2,1)} %get-tuple-element.42), channel_id=1, source_target_pairs={{0,2},{2,4},{4,6},{6,0},{1,3},{3,5},{5,7},{7,1}} | collective-permute-start | bytes 14155784 | tf_op jit(solution)/shard_map/ppermute | solution.py:73
  2315.5 304.6 %collective-permute-start.30 = (bf16[3072,768]{1,0:T(8,128)(2,1)}, bf16[3072,768]{1,0:T(8,128)(2,1)}, u32[]{:S(2)}, u32[]{:S(2)}) collective-permute-start(bf16[3072,768]{1,0:T(8,128)(2,1)} %get-tuple-element.42), channel_id=1, source_target_pairs={{0,1},{1,0},{2,3},{3,2},{4,5},{5,4},{6,7},{7,6}} | collective-permute-start | bytes 14155784 | tf_op jit(solution)/shard_map/ppermute | solution.py:71
  2315.5 404.5 %collective-permute-start.25 = (bf16[768,3072]{1,0:T(8,128)(2,1)}, bf16[768,3072]{1,0:T(8,128)(2,1)}, u32[]{:S(2)}, u32[]{:S(2)}) collective-permute-start(bf16[768,3072]{1,0:T(8,128)(2,1)} %get-tuple-element.38), channel_id=1, source_target_pairs={{0,2},{2,4},{4,6},{6,0},{1,3},{3,5},{5,7},{7,1}} | collective-permute-start | bytes 14155784 | tf_op jit(solution)/shard_map/ppermute | solution.py:73
  2415.7 304.2 %collective-permute-start.24 = (bf16[768,3072]{1,0:T(8,128)(2,1)}, bf16[768,3072]{1,0:T(8,128)(2,1)}, u32[]{:S(2)}, u32[]{:S(2)}) collective-permute-start(bf16[768,3072]{1,0:T(8,128)(2,1)} %get-tuple-element.38), channel_id=1, source_target_pairs={{0,1},{1,0},{2,3},{3,2},{4,5},{5,4},{6,7},{7,6}} | collective-permute-start | bytes 14155784 | tf_op jit(solution)/shard_map/ppermute | solution.py:71
  2516.9 303.4 %collective-permute-start.29 = (bf16[768,3072]{1,0:T(8,128)(2,1)}, bf16[768,3072]{1,0:T(8,128)(2,1)S(1)}, u32[]{:S(2)}, u32[]{:S(2)}) collective-permute-start(bf16[768,3072]{1,0:T(8,128)(2,1)} %get-tuple-element.34), channel_id=1, source_target_pairs={{0,6},{2,0},{4,2},{6,4},{1,7},{3,1},{5,3},{7,5}} | collective-permute-start | bytes 14155784 | tf_op jit(solution)/shard_map/ppermute | solution.py:74
  2618.9 300.5 %collective-permute-start.28 = (bf16[768,3072]{1,0:T(8,128)(2,1)}, bf16[768,3072]{1,0:T(8,128)(2,1)}, u32[]{:S(2)}, u32[]{:S(2)}) collective-permute-start(bf16[768,3072]{1,0:T(8,128)(2,1)} %get-tuple-element.34), channel_id=1, source_target_pairs={{0,2},{2,4},{4,6},{6,0},{1,3},{3,5},{5,7},{7,1}} | collective-permute-start | bytes 14155784 | tf_op jit(solution)/shard_map/ppermute | solution.py:73
  2620.1 299.2 %collective-permute-start.27 = (bf16[768,3072]{1,0:T(8,128)(2,1)}, bf16[768,3072]{1,0:T(8,128)(2,1)}, u32[]{:S(2)}, u32[]{:S(2)}) collective-permute-start(bf16[768,3072]{1,0:T(8,128)(2,1)} %get-tuple-element.34), channel_id=1, source_target_pairs={{0,1},{1,0},{2,3},{3,2},{4,5},{5,4},{6,7},{7,6}} | collective-permute-start | bytes 14155784 | tf_op jit(solution)/shard_map/ppermute | solution.py:71
  (39 other events, 3899.3 us)
where the time goes:
time: 2940 us; the launch traced here: 2930 us
  waiting for transfers between devices  2020 us (69%)
  matrix products  698 us (24%)
  other arithmetic  136 us (5%)
  local copies, waits for them, and re-layouts  37.6 us (1%)
  starting transfers between devices  36.9 us (1%)
    ppermute x12, waiting for transfers between devices, device_fn(): recv_rp = lax.ppermute(wire_vals, 'row', from_row_prev)  1140 us
    ppermute x12, waiting for transfers between devices, device_fn(): recv_rn = lax.ppermute(wire_vals, 'row', from_row_next)  882 us
    dot_general x6, matrix products, local_grads(): jnp.einsum('bd,bf->df', normed_lo, d_pre, preferred_element_type=jnp.floa...  174 us
    dot_general x6, matrix products, local_grads(): jnp.einsum('bf,bd->fd', act_lo, d_lo, preferred_element_type=jnp.float32)  152 us
    dot_general x6, matrix products, local_grads(): jnp.dot(normed_lo, one_lo[layer_idx], preferred_element_type=jnp.float32)  125 us
    dot_general x6, matrix products, local_grads(): jnp.dot(act_lo, two_lo[layer_idx], preferred_element_type=jnp.float32)  104 us
    dot_general x3, matrix products, local_grads(): jnp.einsum('bd,fd->bf', d_lo, two_lo[layer_idx], preferred_element_type=j...  95.5 us
    div x6, other arithmetic, device_fn(): (own_val + cp_val.astype(jnp.float32) + cn_val.astype(jnp.float32) + rp_v...  66 us
  transfers between devices with their start and end apart: 36, of which 20 were waited for; matrix products, arithmetic and copies ran while one was open for 14% of the time, Pallas kernels for 0%

commit v1 on v0

v1 whole, which is shorter than its diff:
```python
import jax
import jax.numpy as jnp
from jax import lax
from jax.experimental import pallas as pl
from jax.experimental.pallas import tpu as pltpu
from jax.sharding import PartitionSpec as P


LEARN_RATE = 1.5
NORM_EPS = 1e-6
GELU_C = 0.7978845608028654
GELU_K = 0.044715

BF = jnp.bfloat16
F32 = jnp.float32
VMEM_LIMIT = 60 * 1024 * 1024
ROWS = 256
KROWS = 512
SUB = 256


ANY = pl.BlockSpec(memory_space=pl.ANY)


def nn(lhs, rhs):
    return lax.dot_general(lhs, rhs, (((1,), (0,)), ((), ())), preferred_element_type=F32)


def nt(lhs, rhs):
    return lax.dot_general(lhs, rhs, (((1,), (1,)), ((), ())), preferred_element_type=F32)


def view(arr, lead, shape, row_blk=0, col_blk=0):
    return (arr, lead, shape, row_blk, col_blk)


def whole(v):
    _, lead, shape, rb, cb = v
    return pl.BlockSpec((None,) * len(lead) + shape, lambda i: lead + (rb, cb))


def by_rows(v, rows):
    _, lead, shape, rb, cb = v
    steps = shape[0] // rows
    return pl.BlockSpec((None,) * len(lead) + (rows, shape[1]), lambda i: lead + (rb * steps + i, cb))


def run(kernel, grid, ins, outs, aliases=None, scratch=(), flops=0, nbytes=0):
    return pl.pallas_call(
        kernel,
        grid=(grid,),
        in_specs=[spec for _, spec in ins],
        out_specs=[spec for _, spec in outs],
        out_shape=[shape for shape, _ in outs],
        input_output_aliases=aliases or {},
        scratch_shapes=list(scratch),
        compiler_params=pltpu.CompilerParams(dimension_semantics=("arbitrary",), vmem_limit_bytes=VMEM_LIMIT),
        cost_estimate=pl.CostEstimate(flops=int(flops), bytes_accessed=int(nbytes), transcendentals=0),
    )(*[v[0] if isinstance(v, tuple) else v for v, _ in ins])


def norm_of(h):
    x = h.astype(F32)
    inv = lax.rsqrt(jnp.mean(x * x, axis=-1, keepdims=True) + NORM_EPS)
    return x * inv, inv


def fwd_one(h, units, prev, off):
    rows, d = h[2]
    width = units[0][2][1]
    f = 4 * width
    nu = len(units)

    def kernel(h_ref, *refs):
        w_refs, (a_ref, s_ref) = refs[:nu], refs[-2:]
        n, _ = norm_of(h_ref[...])
        n = n.astype(BF)
        for j in range(nu):
            for c in range(0, width, SUB):
                z = nn(n, w_refs[j][:, c:c + SUB].astype(BF))
                t = jnp.tanh(GELU_C * (z + GELU_K * z * z * z))
                cols = slice(j * width + c, j * width + c + SUB)
                a_ref[:, cols] = (0.5 * z * (1.0 + t)).astype(BF)
                s_ref[:, cols] = 0.5 * (1.0 + t) + 0.5 * z * (1.0 - t * t) * GELU_C * (1.0 + 3.0 * GELU_K * z * z)

    blk = pl.BlockSpec((ROWS, nu * width), lambda i: (i, off // nu))
    ins = [(h, by_rows(h, ROWS))] + [(u, whole(u)) for u in units]
    aliases = None
    if prev is not None:
        aliases = {len(ins): 0, len(ins) + 1: 1}
        ins += [(p, ANY) for p in prev]
    return run(kernel, rows // ROWS, ins, [(jax.ShapeDtypeStruct((rows, f), BF), blk), (jax.ShapeDtypeStruct((rows, f), F32), blk)],
               aliases, flops=2 * rows * d * width * nu, nbytes=6 * rows * width * nu)


def fwd_two(h, a, units):
    rows, d = h[2]
    nu = len(units)
    f = a.shape[1]
    part = f // nu
    av = view(a, (), (rows, f))

    def kernel(h_ref, a_ref, *refs):
        w_refs, o_ref = refs[:nu], refs[nu]
        for c in range(0, d, SUB):
            acc = nn(a_ref[:, :part], w_refs[0][:, c:c + SUB].astype(BF))
            for j in range(1, nu):
                acc += nn(a_ref[:, j * part:(j + 1) * part], w_refs[j][:, c:c + SUB].astype(BF))
            o_ref[:, c:c + SUB] = (h_ref[:, c:c + SUB].astype(F32) + acc).astype(BF)

    ov = view(None, (), (rows, d))
    return run(kernel, rows // ROWS, [(h, by_rows(h, ROWS)), (av, by_rows(av, ROWS))] + [(u, whole(u)) for u in units],
               [(jax.ShapeDtypeStruct((rows, d), BF), by_rows(ov, ROWS))], flops=2 * rows * d * f, nbytes=2 * rows * f)[0]


def fwd_loss(h, a, unit, target, idx, d):
    rows, f = a.shape
    w = unit[2][1]
    scale = 2.0 / (rows * d)
    hv = view(h, (), (rows, w), 0, idx)
    tv = (target[0], target[1], (rows, w), 0, idx)
    av = view(a, (), (rows, f))

    def kernel(h_ref, t_ref, a_ref, w_ref, e_ref, b_ref):
        out = (h_ref[...].astype(F32) + nn(a_ref[...], w_ref[...].astype(BF))).astype(BF)
        e = scale * (out.astype(F32) - t_ref[...].astype(F32))
        e_ref[...] = e
        b_ref[...] = e.astype(BF)

    ov = view(None, (), (rows, w))
    return run(kernel, rows // ROWS, [(hv, by_rows(hv, ROWS)), (tv, by_rows(tv, ROWS)), (av, by_rows(av, ROWS)), (unit, whole(unit))],
               [(jax.ShapeDtypeStruct((rows, w), F32), by_rows(ov, ROWS)), (jax.ShapeDtypeStruct((rows, w), BF), by_rows(ov, ROWS))],
               flops=2 * rows * w * f, nbytes=2 * rows * f)


def back_act(errs, units, slope):
    rows, f = slope.shape
    ne, nu = len(errs), len(units)
    per = units[0][2][0]

    def kernel(*refs):
        e_refs, w_refs = refs[:ne], refs[ne:ne + nu]
        s_ref, o_ref = refs[ne + nu:]
        for c in range(0, f, SUB):
            if ne > 1:
                u = nt(e_refs[0][...], w_refs[0][c:c + SUB, :].astype(BF))
                for k in range(1, ne):
                    u += nt(e_refs[k][...], w_refs[k][c:c + SUB, :].astype(BF))
            else:
                r = c % per
                u = nt(e_refs[0][...], w_refs[c // per][r:r + SUB, :].astype(BF))
            o_ref[:, c:c + SUB] = (u * s_ref[:, c:c + SUB]).astype(BF)

    vs = [view(e, (), e.shape) for e in errs]
    sv = view(slope, (), (rows, f))
    return run(kernel, rows // ROWS, [(v, by_rows(v, ROWS)) for v in vs] + [(u, whole(u)) for u in units] + [(sv, by_rows(sv, ROWS))],
               [(jax.ShapeDtypeStruct((rows, f), BF), by_rows(sv, ROWS))], flops=2 * rows * f * 768, nbytes=6 * rows * f)[0]


def back_norm(dz, units, h, errs):
    rows, f = dz.shape
    d = h[2][1]
    ne, nu = len(errs), len(units)
    per = f // nu

    def kernel(dz_ref, *refs):
        w_refs, h_ref, e_refs, o_ref, m_ref = refs[:nu], refs[nu], refs[nu + 1:nu + 1 + ne], refs[-2], refs[-1]
        for c in range(0, d, SUB):
            m = nt(dz_ref[:, :per], w_refs[0][c:c + SUB, :].astype(BF))
            for j in range(1, nu):
                m += nt(dz_ref[:, j * per:(j + 1) * per], w_refs[j][c:c + SUB, :].astype(BF))
            m_ref[:, c:c + SUB] = m
        n, inv = norm_of(h_ref[...])
        m = m_ref[...]
        back = inv * (m - n * jnp.mean(m * n, axis=-1, keepdims=True))
        w = d // ne
        for k in range(ne):
            o_ref[:, k * w:(k + 1) * w] = (e_refs[k][...] + back[:, k * w:(k + 1) * w]).astype(BF)

    dv = view(dz, (), (rows, f))
    vs = [view(e, (), e.shape) for e in errs]
    ov = view(None, (), (rows, d))
    return run(kernel, rows // ROWS,
               [(dv, by_rows(dv, ROWS))] + [(u, whole(u)) for u in units] + [(h, by_rows(h, ROWS))] + [(v, by_rows(v, ROWS)) for v in vs],
               [(jax.ShapeDtypeStruct((rows, d), BF), by_rows(ov, ROWS))], scratch=[pltpu.VMEM((ROWS, d), F32)],
               flops=2 * rows * f * d, nbytes=2 * rows * f)[0]


def grad_update(small, big, olds, use_norm, flip):
    rows, m = small[2]
    n = big[2][1]
    nu = len(olds)
    per = n // nu
    steps = rows // KROWS

    def kernel(s_ref, b_ref, *refs):
        p_refs, q_refs, w_refs, acc_ref = refs[:nu], refs[nu:2 * nu], refs[2 * nu:3 * nu], refs[-1]
        i = pl.program_id(0)
        s = s_ref[...]
        if use_norm:
            s = norm_of(s)[0].astype(BF)
        st = s.T

        @pl.when(i == 0)
        def _():
            for c in range(0, n, SUB):
                acc_ref[:, c:c + SUB] = nn(st, b_ref[:, c:c + SUB])

        @pl.when(i > 0)
        def _():
            for c in range(0, n, SUB):
                acc_ref[:, c:c + SUB] += nn(st, b_ref[:, c:c + SUB])

        @pl.when(i == steps - 1)
        def _():
            for j in range(nu):
                for c in range(0, per, SUB):
                    g = acc_ref[:, j * per + c:j * per + c + SUB]
                    at = (slice(c, c + SUB), slice(None)) if flip else (slice(None), slice(c, c + SUB))
                    q = p_refs[j][at] - LEARN_RATE * (g.T if flip else g)
                    q_refs[j][at] = q
                    w_refs[j][at] = q.astype(BF)

    def out(u, dt):
        shape = u[2]
        return (jax.ShapeDtypeStruct(shape, dt), pl.BlockSpec(shape, lambda i: (0, 0)))

    res = run(kernel, steps, [(small, by_rows(small, KROWS)), (big, by_rows(big, KROWS))] + [(u, whole(u)) for u in olds],
              [out(u, F32) for u in olds] + [out(u, BF) for u in olds], scratch=[pltpu.VMEM((m, n), F32)],
              flops=2 * rows * m * n, nbytes=10 * m * n)
    return res[:nu], res[nu:]


def combine(even, own, cc, xx, yy, final):
    rows, cols = own.shape
    blk = 256 if cols > 512 else 768

    def kernel(even_ref, q_ref, c_ref, x_ref, y_ref, *refs):
        prev = jnp.where(even_ref[0] == 1, y_ref[...], x_ref[...]).astype(F32)
        nxt = jnp.where(even_ref[0] == 1, x_ref[...], y_ref[...]).astype(F32)
        c = c_ref[...].astype(F32)
        p = (q_ref[...] + c + c + prev + nxt) / 5.0
        if final is None:
            refs[0][...] = p
            refs[1][...] = p.astype(BF)
        else:
            refs[-1][...] = p

    ov = view(None, (), (rows, cols))
    spec = by_rows(ov, blk)
    ins = [(even, pl.BlockSpec(memory_space=pltpu.SMEM))] + [(v, spec) for v in (own, cc, xx, yy)]
    if final is None:
        return run(kernel, rows // blk, ins, [(jax.ShapeDtypeStruct((rows, cols), F32), spec), (jax.ShapeDtypeStruct((rows, cols), BF), spec)],
                   nbytes=18 * rows * cols, flops=8 * rows * cols)
    arr, shape, layer, rb, cb = final
    aliases = None
    if arr is not None:
        aliases = {len(ins): 0}
        ins.append((arr, ANY))
    fv = (None, (0, 0, layer), (rows, cols), rb, cb)
    return run(kernel, rows // blk, ins, [(jax.ShapeDtypeStruct(shape, F32), by_rows(fv, blk))], aliases, nbytes=14 * rows * cols, flops=8 * rows * cols)


X_SWAP = [(0, 1), (1, 0), (2, 3), (3, 2)]
Y_SWAP = [(0, 2), (2, 0), (1, 3), (3, 1)]
C_SWAP = [(0, 1), (1, 0)]

L1B = ["A", "B", "C"]
ONE0 = ["a0", "a1", "a2", "a3"]
TWO0 = ["b0", "b1", "b2", "b3"]
ONE1 = ["d0", "d1", "d2", "d3"]
WIRE = ["A", "B"] + ONE0 + TWO0 + ONE1 + ["C"]
N_STEPS = 3


def graph():
    ops = {}

    def comp(name, us, needs, pri):
        ops[name] = ("tc", us, list(needs), pri)

    for t in range(N_STEPS):
        def w(units):
            return [f"comb{t - 1}_{u}" for u in units] if t else []

        base = t * 1000
        comp(f"f1a{t}_0", 8, w(ONE0[:2]), base + 10)
        comp(f"f1b{t}_0", 8, w(ONE0[2:]) + [f"f1a{t}_0"], base + 11)
        comp(f"f2{t}_0", 13, w(TWO0) + [f"f1b{t}_0"], base + 12)
        comp(f"f1a{t}_1", 8, w(ONE1[:2]) + [f"f2{t}_0"], base + 13)
        comp(f"f1b{t}_1", 8, w(ONE1[2:]) + [f"f1a{t}_1"], base + 14)
        for k, u in enumerate(L1B):
            comp(f"fl{t}_{u}", 6, w([u]) + [f"f1b{t}_1"], base + 20 + (0 if u == "A" else 10 + k))
            comp(f"g2{t}_{u}", 7, [f"fl{t}_{u}"], base + 21 + (0 if u == "A" else 14 + k if u == "B" else 500))
        comp(f"u{t}_1", 13, [f"fl{t}_{u}" for u in L1B] + w(L1B), base + 40)
        comp(f"m{t}", 13, [f"u{t}_1"] + w(ONE1), base + 41)
        comp(f"u{t}_0", 13, [f"m{t}"] + w(TWO0), base + 42)
        for h in (0, 1):
            comp(f"g1{t}_0{h}", 9, [f"u{t}_0"] + w(ONE0[2 * h:2 * h + 2]), base + 50 + h)
            comp(f"g2{t}_0{h}", 9, [f"m{t}"] + w(TWO0[2 * h:2 * h + 2]), base + 60 + h)
            comp(f"g1{t}_1{h}", 9, [f"u{t}_1"] + w(ONE1[2 * h:2 * h + 2]), base + 70 + h)
        made = {u: f"g2{t}_{u}" for u in L1B}
        for h in (0, 1):
            for j in (2 * h, 2 * h + 1):
                made[ONE0[j]], made[TWO0[j]], made[ONE1[j]] = f"g1{t}_0{h}", f"g2{t}_0{h}", f"g1{t}_1{h}"
        for k, u in enumerate(WIRE):
            us = 35.5 if u in L1B else 26.6
            ops[f"x{t}_{u}"] = ("x", us, [made[u]], k)
            ops[f"y{t}_{u}"] = ("y", us, [f"x{t}_{u}"], k)
            ops[f"c{t}_{u}"] = ("c", 3, [made[u]], k)
            comp(f"comb{t}_{u}", 5 if u in L1B else 4, [f"{r}{t}_{u}" for r in "xyc"] + [made[u]], base + 5)
    return ops


DEPTH = 2
MARGIN = 1.5


def plan():
    ops = graph()
    queue = {r: [f"{r}{t}_{u}" for t in range(N_STEPS) for u in WIRE] for r in "xyc"}
    end = {}
    link_end = {r: [] for r in "xyc"}
    order = []
    todo = [n for n in ops if ops[n][0] == "tc"]
    now = 0.0
    while todo or any(queue.values()):
        moved = True
        while moved:
            moved = False
            for r in "ycx":
                while queue[r]:
                    n = queue[r][0]
                    needs = ops[n][2]
                    if not all(d in end and end[d] + (MARGIN if r == "y" else 0) <= now for d in needs):
                        break
                    live = [e for e in link_end[r] if e > now]
                    if len(live) >= DEPTH and r != "c" and False:
                        break
                    begin = max(now, link_end[r][-1] if link_end[r] else 0.0) + 1.0
                    link_end[r].append(begin + ops[n][1])
                    end[n] = link_end[r][-1]
                    order.append(n)
                    queue[r].pop(0)
                    now += 0.7
                    moved = True
        ready = [n for n in todo if all(d in end and end[d] + (MARGIN if d[0] in "xyc" and not d.startswith("comb") else 0) <= now for d in ops[n][2])]
        if ready:
            n = min(ready, key=lambda m: ops[m][3])
            todo.remove(n)
            now += ops[n][1]
            end[n] = now
            order.append(n)
        else:
            later = [e + MARGIN for e in end.values() if e + MARGIN > now + 1e-9]
            now = min(later)
    return order, max(end.values()), end


def solution(mesh):
    def device_fn(w_one, w_two, inputs, targets):
        _, d, f = w_one.shape[2:]
        rows = inputs.shape[3]
        quarter = f // 4
        third = d // 3
        even = (1 - lax.rem(lax.axis_index("row"), 2)).astype(jnp.int32).reshape((1,))
        master, low = {}, {}
        for j in range(4):
            for lay, names in ((0, ONE0), (1, ONE1)):
                master[names[j]] = view(w_one, (0, 0, lay), (d, quarter), 0, j)
            master[TWO0[j]] = view(w_two, (0, 0, 0), (quarter, d), j, 0)
        for j, u in enumerate(L1B):
            master[u] = view(w_two, (0, 0, 1), (f, third), 0, j)
        low.update(master)
        where = {}
        for j in range(4):
            where[ONE0[j]], where[ONE1[j]], where[TWO0[j]] = ("one", 0, 0, j), ("one", 1, 0, j), ("two", 0, j, 0)
        for j, u in enumerate(L1B):
            where[u] = ("two", 1, 0, j)
        final = {"one": None, "two": None}
        shapes = {"one": w_one.shape, "two": w_two.shape}
        st = {}
        own, wire, moved = {}, {}, {}

        def issue(name):
            if name[0] in "xyc" and not name.startswith("comb"):
                r, t, u = name[0], int(name[1]), name.split("_")[1]
                if r == "x":
                    moved[name] = lax.ppermute(wire[t, u], "row", X_SWAP)
                elif r == "y":
                    moved[name] = lax.ppermute(moved[f"x{t}_{u}"], "row", Y_SWAP)
                else:
                    moved[name] = lax.ppermute(wire[t, u], "col", C_SWAP)
                return
            kind, rest = name.split("_")
            t = int(kind[-1])
            kind = kind[:-1]
            x_in = view(inputs, (0, 0, t), (rows, d))
            target = view(targets, (0, 0, t), (rows, d))
            if kind == "comb":
                u = rest
                args = (even, own[t, u], moved[f"c{t}_{u}"], moved[f"x{t}_{u}"], moved[f"y{t}_{u}"])
                if t == N_STEPS - 1:
                    which, layer, rb, cb = where[u]
                    final[which] = combine(*args, (final[which], shapes[which], layer, rb, cb))[0]
                else:
                    p, b = combine(*args, None)
                    master[u], low[u] = view(p, (), p.shape), view(b, (), b.shape)
            elif kind in ("f1a", "f1b"):
                lay = int(rest)
                names = (ONE0, ONE1)[lay]
                h = x_in if lay == 0 else view(st["h", t], (), (rows, d))
                first = kind == "f1a"
                us = names[:2] if first else names[2:]
                prev = None if first else (st["a", t, lay], st["s", t, lay])
                st["a", t, lay], st["s", t, lay] = fwd_one(h, [low[u] for u in us], prev, 0 if first else 2)
            elif kind == "f2":
                st["h", t] = fwd_two(x_in, st["a", t, 0], [low[u] for u in TWO0])
            elif kind == "fl":
                st["e", t, rest], st["eb", t, rest] = fwd_loss(st["h", t], st["a", t, 1], low[rest], target, L1B.index(rest), d)
            elif kind == "u" and rest == "1":
                st["dz", t, 1] = back_act([st["eb", t, u] for u in L1B], [low[u] for u in L1B], st["s", t, 1])
            elif kind == "u":
                st["dz", t, 0] = back_act([st["e0", t]], [low[u] for u in TWO0], st["s", t, 0])
            elif kind == "g2" and rest in L1B:
                eb = st["eb", t, rest]
                a = st["a", t, 1]
                q, b = grad_update(view(eb, (), eb.shape), view(a, (), a.shape), [master[rest]], False, True)
                own[t, rest], wire[t, rest] = q[0], b[0]
            elif kind in ("g1", "g2"):
                lay, half = int(rest[0]), int(rest[1])
                if kind == "g1":
                    names = (ONE0, ONE1)[lay]
                    small = x_in if lay == 0 else view(st["h", t], (), (rows, d))
                    big = view(st["dz", t, lay], (), (rows, f // 2), 0, half)
                else:
                    names = TWO0
                    small = view(st["e0", t], (), (rows, d))
                    big = view(st["a", t, 0], (), (rows, f // 2), 0, half)
                us = names[2 * half:2 * half + 2]
                q, b = grad_update(small, big, [master[u] for u in us], kind == "g1", kind == "g2")
                for k, u in enumerate(us):
                    own[t, u], wire[t, u] = q[k], b[k]

        order = plan()[0]
        for name in order:
            if name.startswith("m") :
                t = int(name[1])
                st["e0", t] = back_norm(st["dz", t, 1], [low[u] for u in ONE1], view(st["h", t], (), (rows, d)), [st["e", t, u] for u in L1B])
            else:
                issue(name)
        return final["one"], final["two"]

    spec = P("row", "col")
    return jax.shard_map(device_fn, mesh=mesh, in_specs=(spec,) * 4, out_specs=(spec, spec), check_vma=False)
```

time: 2940 us -> 2660 us (0.905)
  Pallas kernels: 0 us -> 1140 us
  matrix products: 698 us -> 0 us
  waiting for transfers between devices: 2020 us -> 1400 us
  other arithmetic: 136 us -> 0 us
  starting transfers between devices: 36.9 us -> 93.5 us
  local copies, waits for them, and re-layouts: 37.6 us -> 5.57 us
    pallas_call x0 -> x105, Pallas kernels: none -> 1140 us  [run(): pl.pallas_call(kernel, grid=(grid,), in_specs=[spec for _, spec in ins],...]
    dot_general x30 -> x0, matrix products: 698 us -> none  [the longest x6 174 us: local_grads(): jnp.einsum('bd,bf->df', normed_lo, d_pre, preferred_element_type=jnp.floa...]
    ppermute x36 -> x135, waiting for transfers between devices: 2020 us -> 1400 us  [the longest x45 777 us: issue(): moved[name] = lax.ppermute(wire[t, u], 'row', X_SWAP)]
    div x9 -> x0, other arithmetic: 66 us -> none  [the longest x6 66 us: device_fn(): (own_val + cp_val.astype(jnp.float32) + cn_val.astype(jnp.float32) + rp_v...]
    ppermute x36 -> x135, starting transfers between devices: 36.9 us -> 93.5 us  [the longest x45 53.3 us: issue(): moved[name] = lax.ppermute(wire[t, u], 'row', X_SWAP)]
    another operation x4 -> x0, other arithmetic: 32.6 us -> none  [device_fn(): return (jnp.stack(one_list)[None, None], jnp.stack(two_list)[None, None])]
  transfers between devices with their start and end apart: 36 -> 135, of which waited for: 20 -> 67; matrix products, arithmetic and copies ran while one was open for 14% -> 0% of each run, Pallas kernels for 0% -> 28%
where the time goes in v1:
time: 2660 us; the launch traced here: 2640 us
  waiting for transfers between devices  1400 us (53%)
  Pallas kernels  1140 us (43%)
  starting transfers between devices  93.5 us (4%)
    pallas_call x105, Pallas kernels, run(): pl.pallas_call(kernel, grid=(grid,), in_specs=[spec for _, spec in ins],...  1140 us
    ppermute x45, waiting for transfers between devices, issue(): moved[name] = lax.ppermute(wire[t, u], 'row', X_SWAP)  777 us
    ppermute x45, waiting for transfers between devices, issue(): moved[name] = lax.ppermute(moved[f'x{t}_{u}'], 'row', Y_SWAP)  623 us
    ppermute x45, starting transfers between devices, issue(): moved[name] = lax.ppermute(wire[t, u], 'row', X_SWAP)  53.3 us
  transfers between devices with their start and end apart: 135, of which 67 were waited for; matrix products, arithmetic and copies ran while one was open for 0% of the time, Pallas kernels for 28%

profile of v1, /device:TPU:0, one launch (start us, length us, event | category | flops | bytes accessed | tf_op | source)
XLA Modules:
  0.0 2643.1 jit_solution(12120921397687613664)
XLA Ops:
  464.0 23.4 collective-permute-done.25.x_ref
  500.9 45.5 %collective-permute-done.28.x_ref = bf16[768,768]{1,0:T(8,128)(2,1)} collective-permute-done((bf16[768,768]{1,0:T(8,128)(2,1)}, bf16[768,768]{1,0:T(8,128)(2,1)}, u32[]{:S(2)}, u32[]{:S(2)}) %collective-permute-start.28) | collective-permute-done | bytes 1179680 | tf_op jit(solution)/shard_map/ppermute | solution.py:389
  550.5 28.6 %collective-permute-done.40.x_ref = bf16[3072,256]{1,0:T(8,128)(2,1)S(1)} collective-permute-done((bf16[3072,256]{1,0:T(8,128)(2,1)}, bf16[3072,256]{1,0:T(8,128)(2,1)S(1)}, u32[]{:S(2)}, u32[]{:S(2)}) %collective-permute-start.40) | collective-permute-done | bytes 1572896 | tf_op jit(solution)/shard_map/ppermute | solution.py:389
  602.8 23.3 collective-permute-done.2.y_ref
  653.4 23.3 collective-permute-done.20.y_ref
  678.7 23.3 collective-permute-done.23.y_ref
  1082.3 23.8 collective-permute-done.55.x_ref
  1132.9 23.8 collective-permute-done.49.x_ref
  1183.4 23.8 collective-permute-done.67.x_ref
  1234.1 23.8 collective-permute-done.61.x_ref
  1309.8 23.9 collective-permute-done.70.x_ref
  1346.7 46.0 %collective-permute-done.73.x_ref = bf16[768,768]{1,0:T(8,128)(2,1)} collective-permute-done((bf16[768,768]{1,0:T(8,128)(2,1)}, bf16[768,768]{1,0:T(8,128)(2,1)}, u32[]{:S(2)}, u32[]{:S(2)}) %collective-permute-start.73) | collective-permute-done | bytes 1179680 | tf_op jit(solution)/shard_map/ppermute | solution.py:389
  1421.8 25.3 collective-permute-done.56.y_ref
  1447.1 25.3 collective-permute-done.47.y_ref
  1499.1 23.8 collective-permute-done.65.y_ref
  1523.0 25.3 collective-permute-done.68.y_ref
  1548.2 25.3 collective-permute-done.59.y_ref
  1573.5 25.3 collective-permute-done.62.y_ref
  1943.0 25.2 collective-permute-done.103.x_ref
  1968.2 25.3 collective-permute-done.106.x_ref
  2044.1 25.2 collective-permute-done.118.x_ref
  2069.3 25.4 collective-permute-done.121.x_ref
  2195.8 33.7 %collective-permute-done.115.x_ref = bf16[3072,256]{1,0:T(8,128)(2,1)} collective-permute-done((bf16[3072,256]{1,0:T(8,128)(2,1)}, bf16[3072,256]{1,0:T(8,128)(2,1)}, u32[]{:S(2)}, u32[]{:S(2)}) %collective-permute-start.115) | collective-permute-done | bytes 1572896 | tf_op jit(solution)/shard_map/ppermute | solution.py:389
  2229.5 33.5 %collective-permute-done.130.x_ref = bf16[3072,256]{1,0:T(8,128)(2,1)S(1)} collective-permute-done((bf16[3072,256]{1,0:T(8,128)(2,1)}, bf16[3072,256]{1,0:T(8,128)(2,1)S(1)}, u32[]{:S(2)}, u32[]{:S(2)}) %collective-permute-start.130) | collective-permute-done | bytes 1572896 | tf_op jit(solution)/shard_map/ppermute | solution.py:389
  2292.3 25.1 collective-permute-done.104.y_ref
  2317.4 25.2 collective-permute-done.107.y_ref
  2342.7 25.2 collective-permute-done.125.y_ref
  2368.0 25.2 collective-permute-done.128.y_ref
  2393.3 25.2 collective-permute-done.98.y_ref
  2418.6 92.6 %collective-permute-done.101.y_ref = bf16[768,768]{1,0:T(8,128)(2,1)S(1)} collective-permute-done((bf16[768,768]{1,0:T(8,128)(2,1)}, bf16[768,768]{1,0:T(8,128)(2,1)S(1)}, u32[]{:S(2)}, u32[]{:S(2)}) %collective-permute-start.101) | collective-permute-done | bytes 1179680 | tf_op jit(solution)/shard_map/ppermute | solution.py:391
  2511.2 25.3 collective-permute-done.92.y_ref
  2536.5 25.2 collective-permute-done.95.y_ref
  (437 shorter events, 1721.6 us)
Async XLA Ops:
  550.4 100.9 %collective-permute-start.5 = (bf16[768,768]{1,0:T(8,128)(2,1)}, bf16[768,768]{1,0:T(8,128)(2,1)}, u32[]{:S(2)}, u32[]{:S(2)}) collective-permute-start(bf16[768,768]{1,0:T(8,128)(2,1)} %collective-permute-done.4.x_ref), channel_id=1, source_target_pairs={{0,4},{4,0},{2,6},{6,2},{1,5},{5,1},{3,7},{7,3}} | collective-permute-start | bytes 3538952 | tf_op jit(solution)/shard_map/ppermute | solution.py:391
  580.9 121.0 %collective-permute-start.23 = (bf16[768,768]{1,0:T(8,128)(2,1)}, bf16[768,768]{1,0:T(8,128)(2,1)}, u32[]{:S(2)}, u32[]{:S(2)}) collective-permute-start(bf16[768,768]{1,0:T(8,128)(2,1)} %copy-done.40), channel_id=1, source_target_pairs={{0,4},{4,0},{2,6},{6,2},{1,5},{5,1},{3,7},{7,3}} | collective-permute-start | bytes 3538952 | tf_op jit(solution)/shard_map/ppermute | solution.py:391
  600.8 126.4 %collective-permute-start.14 = (bf16[768,768]{1,0:T(8,128)(2,1)}, bf16[768,768]{1,0:T(8,128)(2,1)}, u32[]{:S(2)}, u32[]{:S(2)}) collective-permute-start(bf16[768,768]{1,0:T(8,128)(2,1)} %collective-permute-done.13.x_ref), channel_id=1, source_target_pairs={{0,4},{4,0},{2,6},{6,2},{1,5},{5,1},{3,7},{7,3}} | collective-permute-start | bytes 3538952 | tf_op jit(solution)/shard_map/ppermute | solution.py:391
  626.1 126.4 %collective-permute-start.17 = (bf16[768,768]{1,0:T(8,128)(2,1)}, bf16[768,768]{1,0:T(8,128)(2,1)}, u32[]{:S(2)}, u32[]{:S(2)}) collective-permute-start(bf16[768,768]{1,0:T(8,128)(2,1)} %collective-permute-done.16.x_ref), channel_id=1, source_target_pairs={{0,4},{4,0},{2,6},{6,2},{1,5},{5,1},{3,7},{7,3}} | collective-permute-start | bytes 3538952 | tf_op jit(solution)/shard_map/ppermute | solution.py:391
  651.4 178.6 %collective-permute-start.37 = (bf16[3072,256]{1,0:T(8,128)(2,1)}, bf16[3072,256]{1,0:T(8,128)(2,1)}, u32[]{:S(2)}, u32[]{:S(2)}) collective-permute-start(bf16[3072,256]{1,0:T(8,128)(2,1)} %get-tuple-element.251), channel_id=1, source_target_pairs={{0,2},{2,0},{4,6},{6,4},{1,3},{3,1},{5,7},{7,5}} | collective-permute-start | bytes 4718600 | tf_op jit(solution)/shard_map/ppermute | solution.py:389
  676.6 153.4 %collective-permute-start.32 = (bf16[768,768]{1,0:T(8,128)(2,1)}, bf16[768,768]{1,0:T(8,128)(2,1)}, u32[]{:S(2)}, u32[]{:S(2)}) collective-permute-start(bf16[768,768]{1,0:T(8,128)(2,1)} %copy-done.35), channel_id=1, source_target_pairs={{0,4},{4,0},{2,6},{6,2},{1,5},{5,1},{3,7},{7,3}} | collective-permute-start | bytes 3538952 | tf_op jit(solution)/shard_map/ppermute | solution.py:391
  701.9 128.6 %collective-permute-start.35 = (bf16[768,768]{1,0:T(8,128)(2,1)}, bf16[768,768]{1,0:T(8,128)(2,1)}, u32[]{:S(2)}, u32[]{:S(2)}) collective-permute-start(bf16[768,768]{1,0:T(8,128)(2,1)} %copy-done.38), channel_id=1, source_target_pairs={{0,4},{4,0},{2,6},{6,2},{1,5},{5,1},{3,7},{7,3}} | collective-permute-start | bytes 3538952 | tf_op jit(solution)/shard_map/ppermute | solution.py:391
  727.2 103.3 %collective-permute-start.26 = (bf16[768,768]{1,0:T(8,128)(2,1)}, bf16[768,768]{1,0:T(8,128)(2,1)}, u32[]{:S(2)}, u32[]{:S(2)}) collective-permute-start(bf16[768,768]{1,0:T(8,128)(2,1)} %collective-permute-done.25.x_ref), channel_id=1, source_target_pairs={{0,4},{4,0},{2,6},{6,2},{1,5},{5,1},{3,7},{7,3}} | collective-permute-start | bytes 3538952 | tf_op jit(solution)/shard_map/ppermute | solution.py:391
  752.5 101.1 %collective-permute-start.29 = (bf16[768,768]{1,0:T(8,128)(2,1)}, bf16[768,768]{1,0:T(8,128)(2,1)}, u32[]{:S(2)}, u32[]{:S(2)}) collective-permute-start(bf16[768,768]{1,0:T(8,128)(2,1)} %collective-permute-done.28.x_ref), channel_id=1, source_target_pairs={{0,4},{4,0},{2,6},{6,2},{1,5},{5,1},{3,7},{7,3}} | collective-permute-start | bytes 3538952 | tf_op jit(solution)/shard_map/ppermute | solution.py:391
  830.0 101.2 %collective-permute-start.39 = (bf16[3072,256]{1,0:T(8,128)(2,1)}, bf16[3072,256]{1,0:T(8,128)(2,1)}, u32[]{:S(2)}, u32[]{:S(2)}) collective-permute-start(bf16[3072,256]{1,0:T(8,128)(2,1)} %get-tuple-element.255), channel_id=1, source_target_pairs={{0,1},{1,0},{2,3},{3,2},{4,5},{5,4},{6,7},{7,6}} | collective-permute-start | bytes 4718600 | tf_op jit(solution)/shard_map/ppermute | solution.py:393
  830.0 129.8 %collective-permute-start.36 = (bf16[3072,256]{1,0:T(8,128)(2,1)}, bf16[3072,256]{1,0:T(8,128)(2,1)}, u32[]{:S(2)}, u32[]{:S(2)}) collective-permute-start(bf16[3072,256]{1,0:T(8,128)(2,1)} %get-tuple-element.251), channel_id=1, source_target_pairs={{0,1},{1,0},{2,3},{3,2},{4,5},{5,4},{6,7},{7,6}} | collective-permute-start | bytes 4718600 | tf_op jit(solution)/shard_map/ppermute | solution.py:393
  830.5 100.7 %collective-permute-start.41 = (bf16[3072,256]{1,0:T(8,128)(2,1)S(1)}, bf16[3072,256]{1,0:T(8,128)(2,1)}, u32[]{:S(2)}, u32[]{:S(2)}) collective-permute-start(bf16[3072,256]{1,0:T(8,128)(2,1)S(1)} %collective-permute-done.40.x_ref), channel_id=1, source_target_pairs={{0,4},{4,0},{2,6},{6,2},{1,5},{5,1},{3,7},{7,3}} | collective-permute-start | bytes 4718600 | tf_op jit(solution)/shard_map/ppermute | solution.py:391
  853.6 106.2 %collective-permute-start.38 = (bf16[3072,256]{1,0:T(8,128)(2,1)}, bf16[3072,256]{1,0:T(8,128)(2,1)}, u32[]{:S(2)}, u32[]{:S(2)}) collective-permute-start(bf16[3072,256]{1,0:T(8,128)(2,1)} %collective-permute-done.37.x_ref), channel_id=1, source_target_pairs={{0,4},{4,0},{2,6},{6,2},{1,5},{5,1},{3,7},{7,3}} | collective-permute-start | bytes 4718600 | tf_op jit(solution)/shard_map/ppermute | solution.py:391
  1394.7 102.9 %collective-permute-start.50 = (bf16[768,768]{1,0:T(8,128)(2,1)}, bf16[768,768]{1,0:T(8,128)(2,1)}, u32[]{:S(2)}, u32[]{:S(2)}) collective-permute-start(bf16[768,768]{1,0:T(8,128)(2,1)} %collective-permute-done.49.x_ref), channel_id=1, source_target_pairs={{0,4},{4,0},{2,6},{6,2},{1,5},{5,1},{3,7},{7,3}} | collective-permute-start | bytes 3538952 | tf_op jit(solution)/shard_map/ppermute | solution.py:391
  1419.1 103.8 %collective-permute-start.65 = (bf16[768,768]{1,0:T(8,128)(2,1)}, bf16[768,768]{1,0:T(8,128)(2,1)}, u32[]{:S(2)}, u32[]{:S(2)}) collective-permute-start(bf16[768,768]{1,0:T(8,128)(2,1)} %copy-done.41), channel_id=1, source_target_pairs={{0,4},{4,0},{2,6},{6,2},{1,5},{5,1},{3,7},{7,3}} | collective-permute-start | bytes 3538952 | tf_op jit(solution)/shard_map/ppermute | solution.py:391
  1421.8 126.4 %collective-permute-start.68 = (bf16[768,768]{1,0:T(8,128)(2,1)}, bf16[768,768]{1,0:T(8,128)(2,1)}, u32[]{:S(2)}, u32[]{:S(2)}) collective-permute-start(bf16[768,768]{1,0:T(8,128)(2,1)} %copy-done.44), channel_id=1, source_target_pairs={{0,4},{4,0},{2,6},{6,2},{1,5},{5,1},{3,7},{7,3}} | collective-permute-start | bytes 3538952 | tf_op jit(solution)/shard_map/ppermute | solution.py:391
  1447.1 126.4 %collective-permute-start.59 = (bf16[768,768]{1,0:T(8,128)(2,1)}, bf16[768,768]{1,0:T(8,128)(2,1)}, u32[]{:S(2)}, u32[]{:S(2)}) collective-permute-start(bf16[768,768]{1,0:T(8,128)(2,1)} %collective-permute-done.58.x_ref), channel_id=1, source_target_pairs={{0,4},{4,0},{2,6},{6,2},{1,5},{5,1},{3,7},{7,3}} | collective-permute-start | bytes 3538952 | tf_op jit(solution)/shard_map/ppermute | solution.py:391
  1472.4 126.4 %collective-permute-start.62 = (bf16[768,768]{1,0:T(8,128)(2,1)}, bf16[768,768]{1,0:T(8,128)(2,1)}, u32[]{:S(2)}, u32[]{:S(2)}) collective-permute-start(bf16[768,768]{1,0:T(8,128)(2,1)} %collective-permute-done.61.x_ref), channel_id=1, source_target_pairs={{0,4},{4,0},{2,6},{6,2},{1,5},{5,1},{3,7},{7,3}} | collective-permute-start | bytes 3538952 | tf_op jit(solution)/shard_map/ppermute | solution.py:391
  1497.7 176.9 %collective-permute-start.82 = (bf16[3072,256]{1,0:T(8,128)(2,1)}, bf16[3072,256]{1,0:T(8,128)(2,1)S(1)}, u32[]{:S(2)}, u32[]{:S(2)}) collective-permute-start(bf16[3072,256]{1,0:T(8,128)(2,1)} %get-tuple-element.323), channel_id=1, source_target_pairs={{0,2},{2,0},{4,6},{6,4},{1,3},{3,1},{5,7},{7,5}} | collective-permute-start | bytes 4718600 | tf_op jit(solution)/shard_map/ppermute | solution.py:389
  1522.9 151.7 %collective-permute-start.77 = (bf16[768,768]{1,0:T(8,128)(2,1)}, bf16[768,768]{1,0:T(8,128)(2,1)}, u32[]{:S(2)}, u32[]{:S(2)}) collective-permute-start(bf16[768,768]{1,0:T(8,128)(2,1)} %copy-done.42), channel_id=1, source_target_pairs={{0,4},{4,0},{2,6},{6,2},{1,5},{5,1},{3,7},{7,3}} | collective-permute-start | bytes 3538952 | tf_op jit(solution)/shard_map/ppermute | solution.py:391
  1548.2 126.9 %collective-permute-start.80 = (bf16[768,768]{1,0:T(8,128)(2,1)}, bf16[768,768]{1,0:T(8,128)(2,1)}, u32[]{:S(2)}, u32[]{:S(2)}) collective-permute-start(bf16[768,768]{1,0:T(8,128)(2,1)} %copy-done.46), channel_id=1, source_target_pairs={{0,4},{4,0},{2,6},{6,2},{1,5},{5,1},{3,7},{7,3}} | collective-permute-start | bytes 3538952 | tf_op jit(solution)/shard_map/ppermute | solution.py:391
  1573.5 103.7 %collective-permute-start.71 = (bf16[768,768]{1,0:T(8,128)(2,1)}, bf16[768,768]{1,0:T(8,128)(2,1)}, u32[]{:S(2)}, u32[]{:S(2)}) collective-permute-start(bf16[768,768]{1,0:T(8,128)(2,1)} %collective-permute-done.70.x_ref), channel_id=1, source_target_pairs={{0,4},{4,0},{2,6},{6,2},{1,5},{5,1},{3,7},{7,3}} | collective-permute-start | bytes 3538952 | tf_op jit(solution)/shard_map/ppermute | solution.py:391
  1674.7 122.3 %collective-permute-start.81 = (bf16[3072,256]{1,0:T(8,128)(2,1)}, bf16[3072,256]{1,0:T(8,128)(2,1)}, u32[]{:S(2)}, u32[]{:S(2)}) collective-permute-start(bf16[3072,256]{1,0:T(8,128)(2,1)} %get-tuple-element.323), channel_id=1, source_target_pairs={{0,1},{1,0},{2,3},{3,2},{4,5},{5,4},{6,7},{7,6}} | collective-permute-start | bytes 4718600 | tf_op jit(solution)/shard_map/ppermute | solution.py:393
  1691.1 105.9 %collective-permute-start.83 = (bf16[3072,256]{1,0:T(8,128)(2,1)S(1)}, bf16[3072,256]{1,0:T(8,128)(2,1)}, u32[]{:S(2)}, u32[]{:S(2)}) collective-permute-start(bf16[3072,256]{1,0:T(8,128)(2,1)S(1)} %collective-permute-done.82.x_ref), channel_id=1, source_target_pairs={{0,4},{4,0},{2,6},{6,2},{1,5},{5,1},{3,7},{7,3}} | collective-permute-start | bytes 4718600 | tf_op jit(solution)/shard_map/ppermute | solution.py:391
  2286.0 107.2 %collective-permute-start.128 = (bf16[768,768]{1,0:T(8,128)(2,1)}, bf16[768,768]{1,0:T(8,128)(2,1)S(1)}, u32[]{:S(2)}, u32[]{:S(2)}) collective-permute-start(bf16[768,768]{1,0:T(8,128)(2,1)} %collective-permute-done.127.x_ref), channel_id=1, source_target_pairs={{0,4},{4,0},{2,6},{6,2},{1,5},{5,1},{3,7},{7,3}} | collective-permute-start | bytes 3538952 | tf_op jit(solution)/shard_map/ppermute | solution.py:391
  2292.2 126.3 %collective-permute-start.98 = (bf16[768,768]{1,0:T(8,128)(2,1)}, bf16[768,768]{1,0:T(8,128)(2,1)S(1)}, u32[]{:S(2)}, u32[]{:S(2)}) collective-permute-start(bf16[768,768]{1,0:T(8,128)(2,1)} %copy-done.17), channel_id=1, source_target_pairs={{0,4},{4,0},{2,6},{6,2},{1,5},{5,1},{3,7},{7,3}} | collective-permute-start | bytes 3538952 | tf_op jit(solution)/shard_map/ppermute | solution.py:391
  2317.4 244.4 %collective-permute-start.131 = (bf16[3072,256]{1,0:T(8,128)(2,1)S(1)}, bf16[3072,256]{1,0:T(8,128)(2,1)S(1)}, u32[]{:S(2)}, u32[]{:S(2)}) collective-permute-start(bf16[3072,256]{1,0:T(8,128)(2,1)S(1)} %collective-permute-done.130.x_ref), channel_id=1, source_target_pairs={{0,4},{4,0},{2,6},{6,2},{1,5},{5,1},{3,7},{7,3}} | collective-permute-start | bytes 4718600 | tf_op jit(solution)/shard_map/ppermute | solution.py:391
  2342.7 220.4 %collective-permute-start.134 = (bf16[3072,256]{1,0:T(8,128)(2,1)S(1)}, bf16[3072,256]{1,0:T(8,128)(2,1)S(1)}, u32[]{:S(2)}, u32[]{:S(2)}) collective-permute-start(bf16[3072,256]{1,0:T(8,128)(2,1)S(1)} %collective-permute-done.133.x_ref), channel_id=1, source_target_pairs={{0,4},{4,0},{2,6},{6,2},{1,5},{5,1},{3,7},{7,3}} | collective-permute-start | bytes 4718600 | tf_op jit(solution)/shard_map/ppermute | solution.py:391
  2368.0 143.2 %collective-permute-start.101 = (bf16[768,768]{1,0:T(8,128)(2,1)}, bf16[768,768]{1,0:T(8,128)(2,1)S(1)}, u32[]{:S(2)}, u32[]{:S(2)}) collective-permute-start(bf16[768,768]{1,0:T(8,128)(2,1)} %collective-permute-done.100.x_ref), channel_id=1, source_target_pairs={{0,4},{4,0},{2,6},{6,2},{1,5},{5,1},{3,7},{7,3}} | collective-permute-start | bytes 3538952 | tf_op jit(solution)/shard_map/ppermute | solution.py:391
  2393.2 143.2 %collective-permute-start.92 = (bf16[768,768]{1,0:T(8,128)(2,1)}, bf16[768,768]{1,0:T(8,128)(2,1)S(1)}, u32[]{:S(2)}, u32[]{:S(2)}) collective-permute-start(bf16[768,768]{1,0:T(8,128)(2,1)} %copy-done.19), channel_id=1, source_target_pairs={{0,4},{4,0},{2,6},{6,2},{1,5},{5,1},{3,7},{7,3}} | collective-permute-start | bytes 3538952 | tf_op jit(solution)/shard_map/ppermute | solution.py:391
  2418.5 143.2 %collective-permute-start.95 = (bf16[768,768]{1,0:T(8,128)(2,1)}, bf16[768,768]{1,0:T(8,128)(2,1)S(1)}, u32[]{:S(2)}, u32[]{:S(2)}) collective-permute-start(bf16[768,768]{1,0:T(8,128)(2,1)} %collective-permute-done.94.x_ref), channel_id=1, source_target_pairs={{0,4},{4,0},{2,6},{6,2},{1,5},{5,1},{3,7},{7,3}} | collective-permute-start | bytes 3538952 | tf_op jit(solution)/shard_map/ppermute | solution.py:391
  2511.2 125.8 %collective-permute-start.114 = (bf16[3072,256]{1,0:T(8,128)(2,1)}, bf16[3072,256]{1,0:T(8,128)(2,1)}, u32[]{:S(2)}, u32[]{:S(2)}) collective-permute-start(bf16[3072,256]{1,0:T(8,128)(2,1)} %get-tuple-element.367), channel_id=1, source_target_pairs={{0,1},{1,0},{2,3},{3,2},{4,5},{5,4},{6,7},{7,6}} | collective-permute-start | bytes 4718600 | tf_op jit(solution)/shard_map/ppermute | solution.py:393
  (150 other events, 10324.3 us)

commit v2 on v1

v2 whole, which is shorter than its diff:
```python
import jax
import jax.numpy as jnp
from jax import lax
from jax.experimental import pallas as pl
from jax.experimental.pallas import tpu as pltpu
from jax.sharding import PartitionSpec as P


LEARN_RATE = 1.5
NORM_EPS = 1e-6
GELU_C = 0.7978845608028654
GELU_K = 0.044715

BF = jnp.bfloat16
F32 = jnp.float32
VMEM_LIMIT = 60 * 1024 * 1024
ROWS = 256
MROWS = 512
LROWS = 1024
KROWS = 512
SUB = 256


ANY = pl.BlockSpec(memory_space=pl.ANY)


def nn(lhs, rhs):
    return lax.dot_general(lhs, rhs, (((1,), (0,)), ((), ())), preferred_element_type=F32)


def nt(lhs, rhs):
    return lax.dot_general(lhs, rhs, (((1,), (1,)), ((), ())), preferred_element_type=F32)


def view(arr, lead, shape, row_blk=0, col_blk=0):
    return (arr, lead, shape, row_blk, col_blk)


def whole(v):
    _, lead, shape, rb, cb = v
    return pl.BlockSpec((None,) * len(lead) + shape, lambda i: lead + (rb, cb))


def by_rows(v, rows):
    _, lead, shape, rb, cb = v
    steps = shape[0] // rows
    return pl.BlockSpec((None,) * len(lead) + (rows, shape[1]), lambda i: lead + (rb * steps + i, cb))


def run(kernel, grid, ins, outs, aliases=None, scratch=(), flops=0, nbytes=0):
    return pl.pallas_call(
        kernel,
        grid=(grid,),
        in_specs=[spec for _, spec in ins],
        out_specs=[spec for _, spec in outs],
        out_shape=[shape for shape, _ in outs],
        input_output_aliases=aliases or {},
        scratch_shapes=list(scratch),
        compiler_params=pltpu.CompilerParams(dimension_semantics=("arbitrary",), vmem_limit_bytes=VMEM_LIMIT),
        cost_estimate=pl.CostEstimate(flops=int(flops), bytes_accessed=int(nbytes), transcendentals=0),
    )(*[v[0] if isinstance(v, tuple) else v for v, _ in ins])


def norm_of(h):
    x = h.astype(F32)
    inv = lax.rsqrt(jnp.mean(x * x, axis=-1, keepdims=True) + NORM_EPS)
    return x * inv, inv


def fwd_one(h, units, prev, off):
    rows, d = h[2]
    width = units[0][2][1]
    f = 4 * width
    nu = len(units)
    rb = ROWS if nu > 1 else 2 * ROWS

    def kernel(h_ref, *refs):
        w_refs, (a_ref, s_ref) = refs[:nu], refs[-2:]
        n, _ = norm_of(h_ref[...])
        n = n.astype(BF)
        for j in range(nu):
            for c in range(0, width, SUB):
                z = nn(n, w_refs[j][:, c:c + SUB].astype(BF))
                z2 = z * z
                t = jnp.tanh(z * (GELU_C + (GELU_C * GELU_K) * z2))
                half = 0.5 + 0.5 * t
                a = z * half
                cols = slice(j * width + c, j * width + c + SUB)
                a_ref[:, cols] = a.astype(BF)
                s_ref[:, cols] = half + a * (1.0 - t) * (GELU_C + (3.0 * GELU_C * GELU_K) * z2)

    blk = pl.BlockSpec((rb, nu * width), lambda i: (i, off // nu))
    ins = [(h, by_rows(h, rb))] + [(u, whole(u)) for u in units]
    aliases = None
    if prev is not None:
        aliases = {len(ins): 0, len(ins) + 1: 1}
        ins += [(p, ANY) for p in prev]
    return run(kernel, rows // rb, ins, [(jax.ShapeDtypeStruct((rows, f), BF), blk), (jax.ShapeDtypeStruct((rows, f), F32), blk)],
               aliases, flops=2 * rows * d * width * nu, nbytes=6 * rows * width * nu)


def fwd_two(h, a, units):
    rows, d = h[2]
    nu = len(units)
    f = a.shape[1]
    part = f // nu
    av = view(a, (), (rows, f))

    def kernel(h_ref, a_ref, *refs):
        w_refs, o_ref = refs[:nu], refs[nu]
        for c in range(0, d, SUB):
            acc = nn(a_ref[:, :part], w_refs[0][:, c:c + SUB].astype(BF))
            for j in range(1, nu):
                acc += nn(a_ref[:, j * part:(j + 1) * part], w_refs[j][:, c:c + SUB].astype(BF))
            o_ref[:, c:c + SUB] = (h_ref[:, c:c + SUB].astype(F32) + acc).astype(BF)

    ov = view(None, (), (rows, d))
    return run(kernel, rows // MROWS, [(h, by_rows(h, MROWS)), (av, by_rows(av, MROWS))] + [(u, whole(u)) for u in units],
               [(jax.ShapeDtypeStruct((rows, d), BF), by_rows(ov, MROWS))], flops=2 * rows * d * f, nbytes=2 * rows * f)[0]


def fwd_loss(h, a, unit, target, idx, d):
    rows, f = a.shape
    w = unit[2][1]
    scale = 2.0 / (rows * d)
    hv = view(h, (), (rows, w), 0, idx)
    tv = (target[0], target[1], (rows, w), 0, idx)
    av = view(a, (), (rows, f))

    def kernel(h_ref, t_ref, a_ref, w_ref, e_ref, b_ref):
        out = (h_ref[...].astype(F32) + nn(a_ref[...], w_ref[...].astype(BF))).astype(BF)
        e = scale * (out.astype(F32) - t_ref[...].astype(F32))
        e_ref[...] = e
        b_ref[...] = e.astype(BF)

    ov = view(None, (), (rows, w))
    return run(kernel, rows // LROWS, [(hv, by_rows(hv, LROWS)), (tv, by_rows(tv, LROWS)), (av, by_rows(av, LROWS)), (unit, whole(unit))],
               [(jax.ShapeDtypeStruct((rows, w), F32), by_rows(ov, LROWS)), (jax.ShapeDtypeStruct((rows, w), BF), by_rows(ov, LROWS))],
               flops=2 * rows * w * f, nbytes=2 * rows * f)


def back_act(errs, units, slope, lo=0, of=1):
    rows, f = slope.shape
    f = f // of
    ne, nu = len(errs), len(units)
    per = units[0][2][0]

    def kernel(*refs):
        e_refs, w_refs = refs[:ne], refs[ne:ne + nu]
        s_ref, o_ref = refs[ne + nu:]
        for c in range(0, f, SUB):
            if ne > 1:
                u = nt(e_refs[0][...], w_refs[0][c:c + SUB, :].astype(BF))
                for k in range(1, ne):
                    u += nt(e_refs[k][...], w_refs[k][c:c + SUB, :].astype(BF))
            else:
                r = c % per
                u = nt(e_refs[0][...], w_refs[c // per][r:r + SUB, :].astype(BF))
            o_ref[:, c:c + SUB] = (u * s_ref[:, c:c + SUB]).astype(BF)

    vs = [view(e, (), e.shape) for e in errs]
    sv = view(slope, (), (rows, f), 0, lo)
    ov = view(None, (), (rows, f))
    return run(kernel, rows // MROWS, [(v, by_rows(v, MROWS)) for v in vs] + [(u, whole(u)) for u in units] + [(sv, by_rows(sv, MROWS))],
               [(jax.ShapeDtypeStruct((rows, f), BF), by_rows(ov, MROWS))], flops=2 * rows * f * 768, nbytes=6 * rows * f)[0]


def back_norm(dz, units, h, errs):
    rows, f = dz.shape
    d = h[2][1]
    ne, nu = len(errs), len(units)
    per = f // nu

    def kernel(dz_ref, *refs):
        w_refs, h_ref, e_refs, o_ref, m_ref = refs[:nu], refs[nu], refs[nu + 1:nu + 1 + ne], refs[-2], refs[-1]
        for c in range(0, d, SUB):
            m = nt(dz_ref[:, :per], w_refs[0][c:c + SUB, :].astype(BF))
            for j in range(1, nu):
                m += nt(dz_ref[:, j * per:(j + 1) * per], w_refs[j][c:c + SUB, :].astype(BF))
            m_ref[:, c:c + SUB] = m
        n, inv = norm_of(h_ref[...])
        m = m_ref[...]
        back = inv * (m - n * jnp.mean(m * n, axis=-1, keepdims=True))
        w = d // ne
        for k in range(ne):
            o_ref[:, k * w:(k + 1) * w] = (e_refs[k][...] + back[:, k * w:(k + 1) * w]).astype(BF)

    dv = view(dz, (), (rows, f))
    vs = [view(e, (), e.shape) for e in errs]
    ov = view(None, (), (rows, d))
    return run(kernel, rows // MROWS,
               [(dv, by_rows(dv, MROWS))] + [(u, whole(u)) for u in units] + [(h, by_rows(h, MROWS))] + [(v, by_rows(v, MROWS)) for v in vs],
               [(jax.ShapeDtypeStruct((rows, d), BF), by_rows(ov, MROWS))], scratch=[pltpu.VMEM((MROWS, d), F32)],
               flops=2 * rows * f * d, nbytes=2 * rows * f)[0]


def grad_update(small, big, olds, cuts, use_norm, flip):
    rows, m = small[2]
    n = big[2][1]
    nu = len(olds)
    per = n // nu
    steps = rows // KROWS
    out_shapes, out_kinds = [], []
    for j, u in enumerate(olds):
        r, c = u[2]
        out_shapes += [((r, c), F32), ((r, c), BF)] + ([((r // cuts[j], c), BF)] * cuts[j] if cuts[j] > 1 else [])
        out_kinds += [(j, -2), (j, -1)] + ([(j, k) for k in range(cuts[j])] if cuts[j] > 1 else [])

    def kernel(s_ref, b_ref, *refs):
        p_refs, o_refs, acc_ref = refs[:nu], refs[nu:-1], refs[-1]
        i = pl.program_id(0)
        s = s_ref[...]
        if use_norm:
            s = norm_of(s)[0].astype(BF)
        st = s.T

        @pl.when(i == 0)
        def _():
            for c in range(0, n, SUB):
                acc_ref[:, c:c + SUB] = nn(st, b_ref[:, c:c + SUB])

        @pl.when(i > 0)
        def _():
            for c in range(0, n, SUB):
                acc_ref[:, c:c + SUB] += nn(st, b_ref[:, c:c + SUB])

        @pl.when(i == steps - 1)
        def _():
            for (j, kind), o_ref in zip(out_kinds, o_refs):
                if kind != -2:
                    continue
                w_ref = o_refs[out_kinds.index((j, -1))]
                pieces = [o_refs[out_kinds.index((j, k))] for k in range(cuts[j])] if cuts[j] > 1 else []
                size = olds[j][2][0] // cuts[j]
                for c in range(0, per, SUB):
                    g = acc_ref[:, j * per + c:j * per + c + SUB]
                    at = (slice(c, c + SUB), slice(None)) if flip else (slice(None), slice(c, c + SUB))
                    q = p_refs[j][at] - LEARN_RATE * (g.T if flip else g)
                    low = q.astype(BF)
                    o_ref[at] = q
                    w_ref[at] = low
                    for k, piece in enumerate(pieces):
                        if flip:
                            if c // size == k:
                                piece[c - k * size:c - k * size + SUB, :] = low
                        else:
                            piece[:, c:c + SUB] = low[k * size:(k + 1) * size]

    res = run(kernel, steps, [(small, by_rows(small, KROWS)), (big, by_rows(big, KROWS))] + [(u, whole(u)) for u in olds],
              [(jax.ShapeDtypeStruct(sh, dt), pl.BlockSpec(sh, lambda i: (0, 0))) for sh, dt in out_shapes],
              scratch=[pltpu.VMEM((m, n), F32)], flops=2 * rows * m * n, nbytes=10 * m * n)
    got = {kind: r for kind, r in zip(out_kinds, res)}
    return [(got[j, -2], got[j, -1], [got[j, k] for k in range(cuts[j])] if cuts[j] > 1 else [got[j, -1]]) for j in range(nu)]


COMB_ROWS = {768: 256, 256: 768}


def combine(even, own, cc, xx, yy, final):
    rows, cols = own.shape
    nc = len(xx)
    blk = rows // nc if nc > 1 else COMB_ROWS[cols]

    def kernel(even_ref, q_ref, c_ref, *refs):
        def mix(x, y):
            prev = jnp.where(even_ref[0] == 1, y, x).astype(F32)
            nxt = jnp.where(even_ref[0] == 1, x, y).astype(F32)
            c = c_ref[...].astype(F32)
            p = (q_ref[...] + c + c + prev + nxt) / 5.0
            if final is None:
                refs[2 * nc][...] = p
                refs[2 * nc + 1][...] = p.astype(BF)
            else:
                refs[-1][...] = p

        if nc == 1:
            mix(refs[0][...], refs[1][...])
        else:
            for k in range(nc):
                @pl.when(pl.program_id(0) == k)
                def _(k=k):
                    mix(refs[k][...], refs[nc + k][...])

    ov = view(None, (), (rows, cols))
    spec = by_rows(ov, blk)
    pv = view(None, (), (rows // nc, cols))
    piece = by_rows(pv, blk) if nc == 1 else whole(pv)
    ins = [(even, pl.BlockSpec(memory_space=pltpu.SMEM)), (own, spec), (cc, spec)] + [(v, piece) for v in list(xx) + list(yy)]
    if final is None:
        return run(kernel, rows // blk, ins, [(jax.ShapeDtypeStruct((rows, cols), F32), spec), (jax.ShapeDtypeStruct((rows, cols), BF), spec)],
                   nbytes=18 * rows * cols, flops=8 * rows * cols)
    arr, shape, layer, rb, cb = final
    aliases = None
    if arr is not None:
        aliases = {len(ins): 0}
        ins.append((arr, ANY))
    fv = (None, (0, 0, layer), (rows, cols), rb, cb)
    return run(kernel, rows // blk, ins, [(jax.ShapeDtypeStruct(shape, F32), by_rows(fv, blk))], aliases, nbytes=14 * rows * cols, flops=8 * rows * cols)


X_SWAP = [(0, 1), (1, 0), (2, 3), (3, 2)]
Y_SWAP = [(0, 2), (2, 0), (1, 3), (3, 1)]
C_SWAP = [(0, 1), (1, 0)]

L1B = ["A", "B", "C"]
ONE0 = ["a0", "a1", "a2", "a3"]
TWO0 = ["b0", "b1", "b2", "b3"]
ONE1 = ["d0", "d1", "d2", "d3"]
N_STEPS = 3
WIRES = [["A"] + ONE1[:2] + ONE0 + TWO0 + ONE1[2:] + ["B", "C"]] * 2 + [["A", "B", "C"] + ONE0 + TWO0 + ONE1]
CUTS = {}
F1_GROUPS = {0: ((0, 1), (2, 3)), 1: ((0, 1), (2,), (3,))}
F1_FIRST = {0: ((0, 1, 2, 3),), 1: ((0, 1, 2, 3),)}
G1_GROUPS = {0: ((0,), (1,), (2, 3)), 1: ((0, 1), (2, 3))}
G2_GROUPS = ((0, 1), (2, 3))
LINK_US = 25.2
START_US = 0.9
MARGIN = 1.5


def pieces(t):
    return [(u, k) for u in WIRES[t] for k in range(CUTS.get(u, 1))]


def f1_groups(t, lay):
    return (F1_GROUPS if t else F1_FIRST)[lay]


def graph():
    ops = {}

    def comp(name, us, needs, pri):
        ops[name] = ("tc", us, list(needs), pri)

    for t in range(N_STEPS):
        def w(units):
            return [f"comb{t - 1}_{u}" for u in units] if t else []

        base = t * 1000
        for lay, names in ((0, ONE0), (1, ONE1)):
            before = [f"f2{t}_0"] if lay else []
            for g, idx in enumerate(f1_groups(t, lay)):
                comp(f"f1{t}_{lay}{g}", {1: 8.8, 2: 13.8, 4: 24.0}[len(idx)] + (0 if t else 2), w([names[j] for j in idx]) + before, base + 10 + 4 * lay + g)
                before = [f"f1{t}_{lay}{g}"]
            if lay == 0:
                comp(f"f2{t}_0", 15, w(TWO0) + before, base + 13)
        for k, u in enumerate(L1B):
            comp(f"fl{t}_{u}", 8.8, w([u]) + before, base + FL_PRI[u])
            comp(f"g2{t}_{u}", 11, [f"fl{t}_{u}"] + w([u]), base + G2_PRI[t][u])
        comp(f"u{t}_1", 19.5, [f"fl{t}_{u}" for u in L1B] + w(L1B), base + 40)
        comp(f"m{t}_0", 17.5, [f"u{t}_1"] + w(ONE1), base + M_PRI)
        for h in (0, 1):
            comp(f"u{t}_0{h}", 11, [f"m{t}_0"] + w(TWO0[2 * h:2 * h + 2]), base + 42 + 10 * h)
        made = {u: f"g2{t}_{u}" for u in L1B}
        for g, idx in enumerate(G1_GROUPS[0]):
            comp(f"g1{t}_0{g}", 14.2 if len(idx) > 1 else 9.5, [f"u{t}_0{j // 2}" for j in idx] + w([ONE0[j] for j in idx]), base + (51, 51.5, 53)[g])
            made.update({ONE0[j]: f"g1{t}_0{g}" for j in idx})
        for g, idx in enumerate(G2_GROUPS):
            comp(f"g2{t}_0{g}", 14.2, [f"m{t}_0"] + w([TWO0[j] for j in idx]), base + 60 + g)
            made.update({TWO0[j]: f"g2{t}_0{g}" for j in idx})
        for g, idx in enumerate(G1_GROUPS[1]):
            comp(f"g1{t}_1{g}", 14.2, [f"u{t}_1"] + w([ONE1[j] for j in idx]), base + G11_PRI[g])
            made.update({ONE1[j]: f"g1{t}_1{g}" for j in idx})
        k = 0
        for u in WIRES[t]:
            n = CUTS.get(u, 1)
            us = LINK_US * (4.0 / 3.0 if u in L1B else 1.0) / n
            for i in range(n):
                ops[f"x{t}_{u}_{i}"] = ("x", us, [made[u]], k)
                ops[f"y{t}_{u}_{i}"] = ("y", us, [f"x{t}_{u}_{i}"], k)
                k += 1
            ops[f"c{t}_{u}"] = ("c", 3, [made[u]], k)
            comp(f"comb{t}_{u}", 6 if u in L1B else 5.5, [f"{r}{t}_{u}_{i}" for r in "xy" for i in range(n)] + [f"c{t}_{u}", made[u]], base + COMB_PRI)
    return ops


FL_PRI = {"A": 20, "B": 22, "C": 24}
G2_PRI = [{"A": 21, "B": 400, "C": 500}] * 2 + [{"A": 21, "B": 23, "C": 25}]
G11_PRI = (40.5, 71)
M_PRI = 41
COMB_PRI = 5


def is_link(name):
    return name[0] in "xyc" and not name.startswith("comb")


def plan():
    ops = graph()
    queue = {r: [f"{r}{t}_{u}_{k}" for t in range(N_STEPS) for u, k in pieces(t)] for r in "xy"}
    queue["c"] = [f"c{t}_{u}" for t in range(N_STEPS) for u in WIRES[t]]
    end = {}
    free = dict.fromkeys("xyc", 0.0)
    order = []
    todo = [n for n in ops if ops[n][0] == "tc"]
    now = 0.0

    def ready_at(n):
        return max([end[d] + (MARGIN if is_link(d) else 0.0) if d in end else 1e9 for d in ops[n][2]], default=0.0)

    while todo or any(queue.values()):
        moved = True
        while moved:
            moved = False
            for r in "yxc":
                while queue[r] and ready_at(queue[r][0]) <= now + 1e-6:
                    n = queue[r].pop(0)
                    now += START_US
                    free[r] = max(now, free[r]) + ops[n][1]
                    end[n] = free[r] + 1.0
                    order.append(n)
                    moved = True
        ready = [n for n in todo if ready_at(n) <= now + 1e-6]
        if ready:
            n = min(ready, key=lambda m: ops[m][3])
            todo.remove(n)
            now += ops[n][1]
            end[n] = now
            order.append(n)
        elif todo or any(queue.values()):
            now = min(x for x in [ready_at(n) for n in todo] + [ready_at(q[0]) for q in queue.values() if q] if x > now)
    return order, max(end.values()), end


def solution(mesh):
    def device_fn(w_one, w_two, inputs, targets):
        _, d, f = w_one.shape[2:]
        rows = inputs.shape[3]
        quarter, third = f // 4, d // 3
        even = (1 - lax.rem(lax.axis_index("row"), 2)).astype(jnp.int32).reshape((1,))
        names = {0: ONE0, 1: ONE1}
        master, where = {}, {}
        for j in range(4):
            for lay in (0, 1):
                where[names[lay][j]] = ("one", lay, (d, quarter), 0, j)
            where[TWO0[j]] = ("two", 0, (quarter, d), j, 0)
        for j, u in enumerate(L1B):
            where[u] = ("two", 1, (f, third), 0, j)
        src = {"one": w_one, "two": w_two}
        for u, (which, lay, shape, rb, cb) in where.items():
            master[u] = view(src[which], (0, 0, lay), shape, rb, cb)
        low = dict(master)
        final = {"one": None, "two": None}
        st, own, wire, cut, moved = {}, {}, {}, {}, {}

        def keep(t, units, got):
            for u, (q, b, parts) in zip(units, got):
                own[t, u], wire[t, u], cut[t, u] = q, b, parts

        def issue(name):
            part = name.split("_")
            t, kind, rest = int(part[0][-1]), part[0][:-1], part[1]
            x_in = view(inputs, (0, 0, t), (rows, d))
            hidden = lambda lay: x_in if lay == 0 else view(st["h", t], (), (rows, d))
            if kind == "x":
                moved[name] = lax.ppermute(cut[t, rest][int(part[2])], "row", X_SWAP)
            elif kind == "y":
                moved[name] = lax.ppermute(moved["x" + name[1:]], "row", Y_SWAP)
            elif kind == "c":
                moved[name] = lax.ppermute(wire[t, rest], "col", C_SWAP)
            elif kind == "comb":
                n = CUTS.get(rest, 1)
                xx, yy = [[moved[f"{r}{t}_{rest}_{k}"] for k in range(n)] for r in "xy"]
                args = (even, own[t, rest], moved[f"c{t}_{rest}"], xx, yy)
                if t == N_STEPS - 1:
                    which, lay, _, rb, cb = where[rest]
                    final[which] = combine(*args, (final[which], src[which].shape, lay, rb, cb))[0]
                else:
                    p, b = combine(*args, None)
                    master[rest], low[rest] = view(p, (), p.shape), view(b, (), b.shape)
            elif kind == "f1":
                lay, g = int(rest[0]), int(rest[1])
                idx = f1_groups(t, lay)[g]
                prev = (st["a", t, lay], st["s", t, lay]) if g else None
                st["a", t, lay], st["s", t, lay] = fwd_one(hidden(lay), [low[names[lay][j]] for j in idx], prev, idx[0])
            elif kind == "f2":
                st["h", t] = fwd_two(x_in, st["a", t, 0], [low[u] for u in TWO0])
            elif kind == "fl":
                target = view(targets, (0, 0, t), (rows, d))
                st["e", t, rest], st["eb", t, rest] = fwd_loss(st["h", t], st["a", t, 1], low[rest], target, L1B.index(rest), d)
            elif kind == "u" and rest == "1":
                st["dz", t, 1] = back_act([st["eb", t, u] for u in L1B], [low[u] for u in L1B], st["s", t, 1])
            elif kind == "u":
                g = int(rest[1])
                st["dz", t, 0, g] = back_act([st["e0", t]], [low[u] for u in TWO0[2 * g:2 * g + 2]], st["s", t, 0], g, 2)
            elif kind == "m":
                st["e0", t] = back_norm(st["dz", t, 1], [low[u] for u in ONE1], hidden(1), [st["e", t, u] for u in L1B])
            elif kind == "g2" and rest in L1B:
                eb, a = st["eb", t, rest], st["a", t, 1]
                keep(t, [rest], grad_update(view(eb, (), eb.shape), view(a, (), a.shape), [master[rest]], [CUTS.get(rest, 1)], False, True))
            else:
                lay, g = int(rest[0]), int(rest[1])
                idx = G1_GROUPS[lay][g] if kind == "g1" else G2_GROUPS[g]
                us = [(names[lay] if kind == "g1" else TWO0)[j] for j in idx]
                n = len(idx)
                if kind == "g2":
                    small, big = view(st["e0", t], (), (rows, d)), view(st["a", t, 0], (), (rows, n * quarter), 0, idx[0] // n)
                elif lay == 1:
                    small, big = hidden(1), view(st["dz", t, 1], (), (rows, n * quarter), 0, idx[0] // n)
                else:
                    small, big = x_in, view(st["dz", t, 0, idx[0] // 2], (), (rows, n * quarter), 0, (idx[0] % 2) // n)
                keep(t, us, grad_update(small, big, [master[u] for u in us], [CUTS.get(u, 1) for u in us], kind == "g1", kind == "g2"))

        for name in plan()[0]:
            issue(name)
        return final["one"], final["two"]

    spec = P("row", "col")
    return jax.shard_map(device_fn, mesh=mesh, in_specs=(spec,) * 4, out_specs=(spec, spec), check_vma=False)
```

time: 2660 us -> 2570 us (0.966)
  waiting for transfers between devices: 1400 us -> 1320 us
  starting transfers between devices: 93.5 us -> 137 us
  Pallas kernels: 1140 us -> 1100 us
    ppermute x135, waiting for transfers between devices: 1400 us -> 1320 us  [the longest x45 677 us: issue(): moved[name] = lax.ppermute(cut[t, rest][int(part[2])], 'row', X_SWAP)]
    ppermute x135, starting transfers between devices: 93.5 us -> 137 us  [the longest x45 82.8 us: issue(): moved[name] = lax.ppermute(cut[t, rest][int(part[2])], 'row', X_SWAP)]
    pallas_call x105 -> x111, Pallas kernels: 1140 us -> 1100 us  [run(): pl.pallas_call(kernel, grid=(grid,), in_specs=[spec for _, spec in ins],...]
  transfers between devices with their start and end apart: 135 -> 135, of which waited for: 67 -> 66; matrix products, arithmetic and copies ran while one was open for 0% -> 0% of each run, Pallas kernels for 28% -> 31%
where the time goes in v2:
time: 2570 us; the launch traced here: 2560 us
  waiting for transfers between devices  1320 us (51%)
  Pallas kernels  1100 us (43%)
  starting transfers between devices  137 us (5%)
    pallas_call x111, Pallas kernels, run(): pl.pallas_call(kernel, grid=(grid,), in_specs=[spec for _, spec in ins],...  1100 us
    ppermute x45, waiting for transfers between devices, issue(): moved[name] = lax.ppermute(cut[t, rest][int(part[2])], 'row', X_SWAP)  677 us
    ppermute x45, waiting for transfers between devices, issue(): moved[name] = lax.ppermute(moved['x' + name[1:]], 'row', Y_SWAP)  639 us
    ppermute x45, starting transfers between devices, issue(): moved[name] = lax.ppermute(cut[t, rest][int(part[2])], 'row', X_SWAP)  82.8 us
    ppermute x45, starting transfers between devices, issue(): moved[name] = lax.ppermute(moved['x' + name[1:]], 'row', Y_SWAP)  51.6 us
  transfers between devices with their start and end apart: 135, of which 66 were waited for; matrix products, arithmetic and copies ran while one was open for 0% of the time, Pallas kernels for 31%

profile of v2, /device:TPU:0, one launch (start us, length us, event | category | flops | bytes accessed | tf_op | source)
XLA Modules:
  0.0 2561.2 jit_solution(6115684594016464200)
XLA Ops:
  0.6 28.0 %shard_map.59 = (bf16[2048,3072]{1,0:T(8,128)(2,1)}, f32[2048,3072]{1,0:T(8,128)}) custom-call(bf16[1,1,3,2048,768]{4,3,2,1,0:T(8,128)(2,1)} %s_ref.17, f32[1,1,2,768,3072]{4,3,2,1,0:T(8,128)} %refs_1_.21, f32[1,1,2,768,3072]{4,3,2,1,0:T(8,128)} %refs_1_.21, f32[1,1,2,768,3072]{4,3,2,1,0:T(8,128)} %refs_1_.21, f32[1,1,2,768,3072]{4,3,2,1,0:T(8,128)} %refs_1_.21), custom_call_target="tpu_custom_call" | custom-call | flops 9663676416 | bytes 37748736 | tf_op jit(solution)/shard_map/pallas_call | solution.py:51
  45.0 28.2 %shard_map.61 = (bf16[2048,3072]{1,0:T(8,128)(2,1)}, f32[2048,3072]{1,0:T(8,128)}) custom-call(bf16[2048,768]{1,0:T(8,128)(2,1)} %shard_map.60.h_ref.refs_4_.s_ref, f32[1,1,2,768,3072]{4,3,2,1,0:T(8,128)} %refs_1_.21, f32[1,1,2,768,3072]{4,3,2,1,0:T(8,128)} %refs_1_.21, f32[1,1,2,768,3072]{4,3,2,1,0:T(8,128)} %refs_1_.21, f32[1,1,2,768,3072]{4,3,2,1,0:T(8,128)} %refs_1_.21), custom_call_target="tpu_custom_call" | custom-call | flops 9663676416 | bytes 37748736 | tf_op jit(solution)/shard_map/pallas_call | solution.py:51
  300.0 23.3 collective-permute-done.22.refs_0_
  426.4 23.4 collective-permute-done.25.refs_0_
  463.3 45.4 %collective-permute-done.28.refs_0_ = bf16[768,768]{1,0:T(8,128)(2,1)} collective-permute-done((bf16[768,768]{1,0:T(8,128)(2,1)}, bf16[768,768]{1,0:T(8,128)(2,1)}, u32[]{:S(2)}, u32[]{:S(2)}) %collective-permute-start.28) | collective-permute-done | bytes 1179680 | tf_op jit(solution)/shard_map/ppermute | solution.py:456
  512.8 28.6 %collective-permute-done.40.refs_0_ = bf16[3072,256]{1,0:T(8,128)(2,1)S(1)} collective-permute-done((bf16[3072,256]{1,0:T(8,128)(2,1)}, bf16[3072,256]{1,0:T(8,128)(2,1)S(1)}, u32[]{:S(2)}, u32[]{:S(2)}) %collective-permute-start.40) | collective-permute-done | bytes 1572896 | tf_op jit(solution)/shard_map/ppermute | solution.py:456
  565.2 23.3 collective-permute-done.11.refs_1_
  615.7 23.3 collective-permute-done.20.refs_1_
  641.0 23.3 collective-permute-done.23.refs_1_
  666.3 23.3 collective-permute-done.14.refs_1_
  691.6 23.3 collective-permute-done.17.refs_1_
  1011.8 23.7 collective-permute-done.67.refs_0_
  1087.7 23.6 collective-permute-done.76.refs_0_
  1239.4 23.7 collective-permute-done.46.refs_0_
  1276.4 45.7 %collective-permute-done.49.refs_0_ = bf16[768,768]{1,0:T(8,128)(2,1)} collective-permute-done((bf16[768,768]{1,0:T(8,128)(2,1)}, bf16[768,768]{1,0:T(8,128)(2,1)}, u32[]{:S(2)}, u32[]{:S(2)}) %collective-permute-start.49) | collective-permute-done | bytes 1179680 | tf_op jit(solution)/shard_map/ppermute | solution.py:456
  1326.2 24.6 collective-permute-done.85.refs_0_
  1352.7 23.8 collective-permute-done.68.refs_1_
  1376.5 25.3 collective-permute-done.59.refs_1_
  1428.6 23.7 collective-permute-done.56.refs_1_
  1452.4 25.3 collective-permute-done.53.refs_1_
  1477.7 25.3 collective-permute-done.47.refs_1_
  1502.9 25.3 collective-permute-done.50.refs_1_
  1604.1 25.3 collective-permute-done.74.refs_1_
  2088.2 45.0 %collective-permute-done.106.refs_0_ = bf16[768,768]{1,0:T(8,128)(2,1)} collective-permute-done((bf16[768,768]{1,0:T(8,128)(2,1)}, bf16[768,768]{1,0:T(8,128)(2,1)}, u32[]{:S(2)}, u32[]{:S(2)}) %collective-permute-start.106) | collective-permute-done | bytes 1179680 | tf_op jit(solution)/shard_map/ppermute | solution.py:456
  2162.9 25.4 collective-permute-done.133.refs_0_
  2203.4 23.7 collective-permute-done.101.refs_1_
  2228.7 23.7 collective-permute-done.92.refs_1_
  2254.0 23.7 collective-permute-done.95.refs_1_
  2279.3 23.8 collective-permute-done.113.refs_1_
  2304.7 23.6 collective-permute-done.110.refs_1_
  2329.8 124.8 %collective-permute-done.104.refs_1_ = bf16[768,768]{1,0:T(8,128)(2,1)S(1)} collective-permute-done((bf16[768,768]{1,0:T(8,128)(2,1)}, bf16[768,768]{1,0:T(8,128)(2,1)S(1)}, u32[]{:S(2)}, u32[]{:S(2)}) %collective-permute-start.104) | collective-permute-done | bytes 1179680 | tf_op jit(solution)/shard_map/ppermute | solution.py:458
  2456.2 23.7 collective-permute-done.107.refs_1_
  (437 shorter events, 1614.1 us)
Async XLA Ops:
  543.3 121.0 %collective-permute-start.23 = (bf16[768,768]{1,0:T(8,128)(2,1)}, bf16[768,768]{1,0:T(8,128)(2,1)}, u32[]{:S(2)}, u32[]{:S(2)}) collective-permute-start(bf16[768,768]{1,0:T(8,128)(2,1)} %collective-permute-done.22.refs_0_), channel_id=1, source_target_pairs={{0,4},{4,0},{2,6},{6,2},{1,5},{5,1},{3,7},{7,3}} | collective-permute-start | bytes 3538952 | tf_op jit(solution)/shard_map/ppermute | solution.py:458
  563.2 126.4 %collective-permute-start.14 = (bf16[768,768]{1,0:T(8,128)(2,1)}, bf16[768,768]{1,0:T(8,128)(2,1)}, u32[]{:S(2)}, u32[]{:S(2)}) collective-permute-start(bf16[768,768]{1,0:T(8,128)(2,1)} %collective-permute-done.13.refs_0_), channel_id=1, source_target_pairs={{0,4},{4,0},{2,6},{6,2},{1,5},{5,1},{3,7},{7,3}} | collective-permute-start | bytes 3538952 | tf_op jit(solution)/shard_map/ppermute | solution.py:458
  588.5 126.4 %collective-permute-start.17 = (bf16[768,768]{1,0:T(8,128)(2,1)}, bf16[768,768]{1,0:T(8,128)(2,1)}, u32[]{:S(2)}, u32[]{:S(2)}) collective-permute-start(bf16[768,768]{1,0:T(8,128)(2,1)} %collective-permute-done.16.refs_0_), channel_id=1, source_target_pairs={{0,4},{4,0},{2,6},{6,2},{1,5},{5,1},{3,7},{7,3}} | collective-permute-start | bytes 3538952 | tf_op jit(solution)/shard_map/ppermute | solution.py:458
  613.7 174.7 %collective-permute-start.37 = (bf16[3072,256]{1,0:T(8,128)(2,1)}, bf16[3072,256]{1,0:T(8,128)(2,1)}, u32[]{:S(2)}, u32[]{:S(2)}) collective-permute-start(bf16[3072,256]{1,0:T(8,128)(2,1)} %get-tuple-element.249), channel_id=1, source_target_pairs={{0,2},{2,0},{4,6},{6,4},{1,3},{3,1},{5,7},{7,5}} | collective-permute-start | bytes 4718600 | tf_op jit(solution)/shard_map/ppermute | solution.py:456
  639.0 149.4 %collective-permute-start.32 = (bf16[768,768]{1,0:T(8,128)(2,1)}, bf16[768,768]{1,0:T(8,128)(2,1)}, u32[]{:S(2)}, u32[]{:S(2)}) collective-permute-start(bf16[768,768]{1,0:T(8,128)(2,1)} %copy-done.37), channel_id=1, source_target_pairs={{0,4},{4,0},{2,6},{6,2},{1,5},{5,1},{3,7},{7,3}} | collective-permute-start | bytes 3538952 | tf_op jit(solution)/shard_map/ppermute | solution.py:458
  664.3 124.6 %collective-permute-start.35 = (bf16[768,768]{1,0:T(8,128)(2,1)}, bf16[768,768]{1,0:T(8,128)(2,1)}, u32[]{:S(2)}, u32[]{:S(2)}) collective-permute-start(bf16[768,768]{1,0:T(8,128)(2,1)} %copy-done.40), channel_id=1, source_target_pairs={{0,4},{4,0},{2,6},{6,2},{1,5},{5,1},{3,7},{7,3}} | collective-permute-start | bytes 3538952 | tf_op jit(solution)/shard_map/ppermute | solution.py:458
  689.6 101.1 %collective-permute-start.26 = (bf16[768,768]{1,0:T(8,128)(2,1)}, bf16[768,768]{1,0:T(8,128)(2,1)}, u32[]{:S(2)}, u32[]{:S(2)}) collective-permute-start(bf16[768,768]{1,0:T(8,128)(2,1)} %collective-permute-done.25.refs_0_), channel_id=1, source_target_pairs={{0,4},{4,0},{2,6},{6,2},{1,5},{5,1},{3,7},{7,3}} | collective-permute-start | bytes 3538952 | tf_op jit(solution)/shard_map/ppermute | solution.py:458
  714.9 101.1 %collective-permute-start.29 = (bf16[768,768]{1,0:T(8,128)(2,1)}, bf16[768,768]{1,0:T(8,128)(2,1)}, u32[]{:S(2)}, u32[]{:S(2)}) collective-permute-start(bf16[768,768]{1,0:T(8,128)(2,1)} %collective-permute-done.28.refs_0_), channel_id=1, source_target_pairs={{0,4},{4,0},{2,6},{6,2},{1,5},{5,1},{3,7},{7,3}} | collective-permute-start | bytes 3538952 | tf_op jit(solution)/shard_map/ppermute | solution.py:458
  788.4 104.0 %collective-permute-start.39 = (bf16[3072,256]{1,0:T(8,128)(2,1)}, bf16[3072,256]{1,0:T(8,128)(2,1)}, u32[]{:S(2)}, u32[]{:S(2)}) collective-permute-start(bf16[3072,256]{1,0:T(8,128)(2,1)} %get-tuple-element.253), channel_id=1, source_target_pairs={{0,1},{1,0},{2,3},{3,2},{4,5},{5,4},{6,7},{7,6}} | collective-permute-start | bytes 4718600 | tf_op jit(solution)/shard_map/ppermute | solution.py:460
  788.4 127.6 %collective-permute-start.36 = (bf16[3072,256]{1,0:T(8,128)(2,1)}, bf16[3072,256]{1,0:T(8,128)(2,1)}, u32[]{:S(2)}, u32[]{:S(2)}) collective-permute-start(bf16[3072,256]{1,0:T(8,128)(2,1)} %get-tuple-element.249), channel_id=1, source_target_pairs={{0,1},{1,0},{2,3},{3,2},{4,5},{5,4},{6,7},{7,6}} | collective-permute-start | bytes 4718600 | tf_op jit(solution)/shard_map/ppermute | solution.py:460
  790.7 101.7 %collective-permute-start.41 = (bf16[3072,256]{1,0:T(8,128)(2,1)S(1)}, bf16[3072,256]{1,0:T(8,128)(2,1)}, u32[]{:S(2)}, u32[]{:S(2)}) collective-permute-start(bf16[3072,256]{1,0:T(8,128)(2,1)S(1)} %collective-permute-done.40.refs_0_), channel_id=1, source_target_pairs={{0,4},{4,0},{2,6},{6,2},{1,5},{5,1},{3,7},{7,3}} | collective-permute-start | bytes 4718600 | tf_op jit(solution)/shard_map/ppermute | solution.py:458
  1324.2 102.9 %collective-permute-start.62 = (bf16[768,768]{1,0:T(8,128)(2,1)}, bf16[768,768]{1,0:T(8,128)(2,1)}, u32[]{:S(2)}, u32[]{:S(2)}) collective-permute-start(bf16[768,768]{1,0:T(8,128)(2,1)} %collective-permute-done.61.refs_0_), channel_id=1, source_target_pairs={{0,4},{4,0},{2,6},{6,2},{1,5},{5,1},{3,7},{7,3}} | collective-permute-start | bytes 3538952 | tf_op jit(solution)/shard_map/ppermute | solution.py:458
  1350.7 101.6 %collective-permute-start.56 = (bf16[768,768]{1,0:T(8,128)(2,1)}, bf16[768,768]{1,0:T(8,128)(2,1)}, u32[]{:S(2)}, u32[]{:S(2)}) collective-permute-start(bf16[768,768]{1,0:T(8,128)(2,1)} %copy-done.42), channel_id=1, source_target_pairs={{0,4},{4,0},{2,6},{6,2},{1,5},{5,1},{3,7},{7,3}} | collective-permute-start | bytes 3538952 | tf_op jit(solution)/shard_map/ppermute | solution.py:458
  1351.9 125.7 %collective-permute-start.53 = (bf16[768,768]{1,0:T(8,128)(2,1)}, bf16[768,768]{1,0:T(8,128)(2,1)}, u32[]{:S(2)}, u32[]{:S(2)}) collective-permute-start(bf16[768,768]{1,0:T(8,128)(2,1)} %collective-permute-done.52.refs_0_), channel_id=1, source_target_pairs={{0,4},{4,0},{2,6},{6,2},{1,5},{5,1},{3,7},{7,3}} | collective-permute-start | bytes 3538952 | tf_op jit(solution)/shard_map/ppermute | solution.py:458
  1376.5 126.4 %collective-permute-start.47 = (bf16[768,768]{1,0:T(8,128)(2,1)}, bf16[768,768]{1,0:T(8,128)(2,1)}, u32[]{:S(2)}, u32[]{:S(2)}) collective-permute-start(bf16[768,768]{1,0:T(8,128)(2,1)} %collective-permute-done.46.refs_0_), channel_id=1, source_target_pairs={{0,4},{4,0},{2,6},{6,2},{1,5},{5,1},{3,7},{7,3}} | collective-permute-start | bytes 3538952 | tf_op jit(solution)/shard_map/ppermute | solution.py:458
  1401.8 126.4 %collective-permute-start.50 = (bf16[768,768]{1,0:T(8,128)(2,1)}, bf16[768,768]{1,0:T(8,128)(2,1)}, u32[]{:S(2)}, u32[]{:S(2)}) collective-permute-start(bf16[768,768]{1,0:T(8,128)(2,1)} %collective-permute-done.49.refs_0_), channel_id=1, source_target_pairs={{0,4},{4,0},{2,6},{6,2},{1,5},{5,1},{3,7},{7,3}} | collective-permute-start | bytes 3538952 | tf_op jit(solution)/shard_map/ppermute | solution.py:458
  1427.1 172.4 %collective-permute-start.82 = (bf16[3072,256]{1,0:T(8,128)(2,1)}, bf16[3072,256]{1,0:T(8,128)(2,1)S(1)}, u32[]{:S(2)}, u32[]{:S(2)}) collective-permute-start(bf16[3072,256]{1,0:T(8,128)(2,1)} %get-tuple-element.323), channel_id=1, source_target_pairs={{0,2},{2,0},{4,6},{6,4},{1,3},{3,1},{5,7},{7,5}} | collective-permute-start | bytes 4718600 | tf_op jit(solution)/shard_map/ppermute | solution.py:456
  1452.4 147.2 %collective-permute-start.77 = (bf16[768,768]{1,0:T(8,128)(2,1)}, bf16[768,768]{1,0:T(8,128)(2,1)}, u32[]{:S(2)}, u32[]{:S(2)}) collective-permute-start(bf16[768,768]{1,0:T(8,128)(2,1)} %copy-done.26), channel_id=1, source_target_pairs={{0,4},{4,0},{2,6},{6,2},{1,5},{5,1},{3,7},{7,3}} | collective-permute-start | bytes 3538952 | tf_op jit(solution)/shard_map/ppermute | solution.py:458
  1477.6 122.4 %collective-permute-start.80 = (bf16[768,768]{1,0:T(8,128)(2,1)}, bf16[768,768]{1,0:T(8,128)(2,1)}, u32[]{:S(2)}, u32[]{:S(2)}) collective-permute-start(bf16[768,768]{1,0:T(8,128)(2,1)} %copy-done.28), channel_id=1, source_target_pairs={{0,4},{4,0},{2,6},{6,2},{1,5},{5,1},{3,7},{7,3}} | collective-permute-start | bytes 3538952 | tf_op jit(solution)/shard_map/ppermute | solution.py:458
  1502.9 101.1 %collective-permute-start.71 = (bf16[768,768]{1,0:T(8,128)(2,1)}, bf16[768,768]{1,0:T(8,128)(2,1)}, u32[]{:S(2)}, u32[]{:S(2)}) collective-permute-start(bf16[768,768]{1,0:T(8,128)(2,1)} %collective-permute-done.70.refs_0_), channel_id=1, source_target_pairs={{0,4},{4,0},{2,6},{6,2},{1,5},{5,1},{3,7},{7,3}} | collective-permute-start | bytes 3538952 | tf_op jit(solution)/shard_map/ppermute | solution.py:458
  1528.2 101.1 %collective-permute-start.74 = (bf16[768,768]{1,0:T(8,128)(2,1)}, bf16[768,768]{1,0:T(8,128)(2,1)}, u32[]{:S(2)}, u32[]{:S(2)}) collective-permute-start(bf16[768,768]{1,0:T(8,128)(2,1)} %collective-permute-done.73.refs_0_), channel_id=1, source_target_pairs={{0,4},{4,0},{2,6},{6,2},{1,5},{5,1},{3,7},{7,3}} | collective-permute-start | bytes 3538952 | tf_op jit(solution)/shard_map/ppermute | solution.py:458
  1599.5 104.6 %collective-permute-start.84 = (bf16[3072,256]{1,0:T(8,128)(2,1)}, bf16[3072,256]{1,0:T(8,128)(2,1)}, u32[]{:S(2)}, u32[]{:S(2)}) collective-permute-start(bf16[3072,256]{1,0:T(8,128)(2,1)} %get-tuple-element.328), channel_id=1, source_target_pairs={{0,1},{1,0},{2,3},{3,2},{4,5},{5,4},{6,7},{7,6}} | collective-permute-start | bytes 4718600 | tf_op jit(solution)/shard_map/ppermute | solution.py:460
  1599.6 128.0 %collective-permute-start.81 = (bf16[3072,256]{1,0:T(8,128)(2,1)}, bf16[3072,256]{1,0:T(8,128)(2,1)}, u32[]{:S(2)}, u32[]{:S(2)}) collective-permute-start(bf16[3072,256]{1,0:T(8,128)(2,1)} %get-tuple-element.323), channel_id=1, source_target_pairs={{0,1},{1,0},{2,3},{3,2},{4,5},{5,4},{6,7},{7,6}} | collective-permute-start | bytes 4718600 | tf_op jit(solution)/shard_map/ppermute | solution.py:460
  1846.6 101.1 %collective-permute-start.100 = (bf16[768,768]{1,0:T(8,128)(2,1)}, bf16[768,768]{1,0:T(8,128)(2,1)}, u32[]{:S(2)}, u32[]{:S(2)}) collective-permute-start(bf16[768,768]{1,0:T(8,128)(2,1)} %get-tuple-element.348), channel_id=1, source_target_pairs={{0,2},{2,0},{4,6},{6,4},{1,3},{3,1},{5,7},{7,5}} | collective-permute-start | bytes 3538952 | tf_op jit(solution)/shard_map/ppermute | solution.py:456
  2035.1 112.2 %collective-permute-start.127 = (bf16[3072,256]{1,0:T(8,128)(2,1)}, bf16[3072,256]{1,0:T(8,128)(2,1)S(1)}, u32[]{:S(2)}, u32[]{:S(2)}) collective-permute-start(bf16[3072,256]{1,0:T(8,128)(2,1)} %get-tuple-element.379), channel_id=1, source_target_pairs={{0,2},{2,0},{4,6},{6,4},{1,3},{3,1},{5,7},{7,5}} | collective-permute-start | bytes 4718600 | tf_op jit(solution)/shard_map/ppermute | solution.py:456
  2190.4 112.7 %collective-permute-start.113 = (bf16[768,768]{1,0:T(8,128)(2,1)}, bf16[768,768]{1,0:T(8,128)(2,1)}, u32[]{:S(2)}, u32[]{:S(2)}) collective-permute-start(bf16[768,768]{1,0:T(8,128)(2,1)} %collective-permute-done.112.refs_0_), channel_id=1, source_target_pairs={{0,4},{4,0},{2,6},{6,2},{1,5},{5,1},{3,7},{7,3}} | collective-permute-start | bytes 3538952 | tf_op jit(solution)/shard_map/ppermute | solution.py:458
  2201.9 126.4 %collective-permute-start.110 = (bf16[768,768]{1,0:T(8,128)(2,1)}, bf16[768,768]{1,0:T(8,128)(2,1)S(1)}, u32[]{:S(2)}, u32[]{:S(2)}) collective-permute-start(bf16[768,768]{1,0:T(8,128)(2,1)} %collective-permute-done.109.refs_0_), channel_id=1, source_target_pairs={{0,4},{4,0},{2,6},{6,2},{1,5},{5,1},{3,7},{7,3}} | collective-permute-start | bytes 3538952 | tf_op jit(solution)/shard_map/ppermute | solution.py:458
  2227.2 252.8 %collective-permute-start.128 = (bf16[3072,256]{1,0:T(8,128)(2,1)S(1)}, bf16[3072,256]{1,0:T(8,128)(2,1)S(1)}, u32[]{:S(2)}, u32[]{:S(2)}) collective-permute-start(bf16[3072,256]{1,0:T(8,128)(2,1)S(1)} %collective-permute-done.127.refs_0_), channel_id=1, source_target_pairs={{0,4},{4,0},{2,6},{6,2},{1,5},{5,1},{3,7},{7,3}} | collective-permute-start | bytes 4718600 | tf_op jit(solution)/shard_map/ppermute | solution.py:458
  2252.4 230.3 %collective-permute-start.131 = (bf16[3072,256]{1,0:T(8,128)(2,1)}, bf16[3072,256]{1,0:T(8,128)(2,1)}, u32[]{:S(2)}, u32[]{:S(2)}) collective-permute-start(bf16[3072,256]{1,0:T(8,128)(2,1)} %collective-permute-done.130.refs_0_), channel_id=1, source_target_pairs={{0,4},{4,0},{2,6},{6,2},{1,5},{5,1},{3,7},{7,3}} | collective-permute-start | bytes 4718600 | tf_op jit(solution)/shard_map/ppermute | solution.py:458
  2277.7 205.2 %collective-permute-start.134 = (bf16[3072,256]{1,0:T(8,128)(2,1)S(1)}, bf16[3072,256]{1,0:T(8,128)(2,1)S(1)}, u32[]{:S(2)}, u32[]{:S(2)}) collective-permute-start(bf16[3072,256]{1,0:T(8,128)(2,1)S(1)} %collective-permute-done.133.refs_0_), channel_id=1, source_target_pairs={{0,4},{4,0},{2,6},{6,2},{1,5},{5,1},{3,7},{7,3}} | collective-permute-start | bytes 4718600 | tf_op jit(solution)/shard_map/ppermute | solution.py:458
  2303.1 151.6 %collective-permute-start.104 = (bf16[768,768]{1,0:T(8,128)(2,1)}, bf16[768,768]{1,0:T(8,128)(2,1)S(1)}, u32[]{:S(2)}, u32[]{:S(2)}) collective-permute-start(bf16[768,768]{1,0:T(8,128)(2,1)} %collective-permute-done.103.refs_0_), channel_id=1, source_target_pairs={{0,4},{4,0},{2,6},{6,2},{1,5},{5,1},{3,7},{7,3}} | collective-permute-start | bytes 3538952 | tf_op jit(solution)/shard_map/ppermute | solution.py:458
  2328.3 151.7 %collective-permute-start.107 = (bf16[768,768]{1,0:T(8,128)(2,1)}, bf16[768,768]{1,0:T(8,128)(2,1)S(1)}, u32[]{:S(2)}, u32[]{:S(2)}) collective-permute-start(bf16[768,768]{1,0:T(8,128)(2,1)} %collective-permute-done.106.refs_0_), channel_id=1, source_target_pairs={{0,4},{4,0},{2,6},{6,2},{1,5},{5,1},{3,7},{7,3}} | collective-permute-start | bytes 3538952 | tf_op jit(solution)/shard_map/ppermute | solution.py:458
  (147 other events, 10245.4 us)

commit v3 on v2

v3 whole, which is shorter than its diff:
```python
import jax
import jax.numpy as jnp
from jax import lax
from jax.experimental import pallas as pl
from jax.experimental.pallas import tpu as pltpu
from jax.sharding import PartitionSpec as P


LEARN_RATE = 1.5
NORM_EPS = 1e-6
GELU_C = 0.7978845608028654
GELU_K = 0.044715

BF = jnp.bfloat16
F32 = jnp.float32
VMEM_LIMIT = 60 * 1024 * 1024
ROWS = 256
MROWS = 512
LROWS = 1024
BROWS = 256
CROWS = 512
KROWS = 512
SUB = 256


ANY = pl.BlockSpec(memory_space=pl.ANY)


def nn(lhs, rhs):
    return lax.dot_general(lhs, rhs, (((1,), (0,)), ((), ())), preferred_element_type=F32)


def nt(lhs, rhs):
    return lax.dot_general(lhs, rhs, (((1,), (1,)), ((), ())), preferred_element_type=F32)


def gelu_slope(z):
    z2 = z * z
    t = jnp.tanh(z * (GELU_C + (GELU_C * GELU_K) * z2))
    half = 0.5 + 0.5 * t
    return half + z * half * (1.0 - t) * (GELU_C + (3.0 * GELU_C * GELU_K) * z2)


def view(arr, lead, shape, row_blk=0, col_blk=0):
    return (arr, lead, shape, row_blk, col_blk)


def whole(v):
    _, lead, shape, rb, cb = v
    return pl.BlockSpec((None,) * len(lead) + shape, lambda i: lead + (rb, cb))


def by_rows(v, rows):
    _, lead, shape, rb, cb = v
    steps = shape[0] // rows
    return pl.BlockSpec((None,) * len(lead) + (rows, shape[1]), lambda i: lead + (rb * steps + i, cb))


def run(kernel, grid, ins, outs, aliases=None, scratch=(), flops=0, nbytes=0):
    return pl.pallas_call(
        kernel,
        grid=(grid,),
        in_specs=[spec for _, spec in ins],
        out_specs=[spec for _, spec in outs],
        out_shape=[shape for shape, _ in outs],
        input_output_aliases=aliases or {},
        scratch_shapes=list(scratch),
        compiler_params=pltpu.CompilerParams(dimension_semantics=("arbitrary",), vmem_limit_bytes=VMEM_LIMIT),
        cost_estimate=pl.CostEstimate(flops=int(flops), bytes_accessed=int(nbytes), transcendentals=0),
    )(*[v[0] if isinstance(v, tuple) else v for v, _ in ins])


def norm_of(h):
    x = h.astype(F32)
    inv = lax.rsqrt(jnp.mean(x * x, axis=-1, keepdims=True) + NORM_EPS)
    return x * inv, inv


def fwd_one(h, units, prev, off, keep_z):
    rows, d = h[2]
    width = units[0][2][1]
    f = 4 * width
    nu = len(units)
    cast = int(units[0][0].dtype == F32)
    rb = ROWS if nu > 1 else 2 * ROWS

    def kernel(h_ref, *refs):
        w_refs, (a_ref, s_ref) = refs[:nu], refs[-2 - cast:len(refs) - cast]
        if cast:
            low_ref = refs[-1]

            @pl.when(pl.program_id(0) == 0)
            def _():
                for j in range(nu):
                    low_ref[j] = w_refs[j][...].astype(BF)

            w_refs = [low_ref.at[j] for j in range(nu)]
        n, _ = norm_of(h_ref[...])
        n = n.astype(BF)
        for j in range(nu):
            for c in range(0, width, SUB):
                z = nn(n, w_refs[j][:, c:c + SUB])
                z2 = z * z
                t = jnp.tanh(z * (GELU_C + (GELU_C * GELU_K) * z2))
                cols = slice(j * width + c, j * width + c + SUB)
                half = 0.5 + 0.5 * t
                a_ref[:, cols] = (z * half).astype(BF)
                s_ref[:, cols] = z if keep_z else half + z * half * (1.0 - t) * (GELU_C + (3.0 * GELU_C * GELU_K) * z2)

    blk = pl.BlockSpec((rb, nu * width), lambda i: (i, off // nu))
    ins = [(h, by_rows(h, rb))] + [(u, whole(u)) for u in units]
    aliases = None
    if prev is not None:
        aliases = {len(ins): 0, len(ins) + 1: 1}
        ins += [(p, ANY) for p in prev]
    return run(kernel, rows // rb, ins, [(jax.ShapeDtypeStruct((rows, f), BF), blk), (jax.ShapeDtypeStruct((rows, f), F32), blk)],
               aliases, scratch=[pltpu.VMEM((nu, d, width), BF)] * cast, flops=2 * rows * d * width * nu, nbytes=6 * rows * width * nu)


def fwd_two(h, a, units):
    rows, d = h[2]
    nu = len(units)
    f = a.shape[1]
    part = f // nu
    av = view(a, (), (rows, f))

    def kernel(h_ref, a_ref, *refs):
        w_refs, o_ref = refs[:nu], refs[nu]
        for c in range(0, d, SUB):
            acc = nn(a_ref[:, :part], w_refs[0][:, c:c + SUB].astype(BF))
            for j in range(1, nu):
                acc += nn(a_ref[:, j * part:(j + 1) * part], w_refs[j][:, c:c + SUB].astype(BF))
            o_ref[:, c:c + SUB] = (h_ref[:, c:c + SUB].astype(F32) + acc).astype(BF)

    ov = view(None, (), (rows, d))
    return run(kernel, rows // MROWS, [(h, by_rows(h, MROWS)), (av, by_rows(av, MROWS))] + [(u, whole(u)) for u in units],
               [(jax.ShapeDtypeStruct((rows, d), BF), by_rows(ov, MROWS))], flops=2 * rows * d * f, nbytes=2 * rows * f)[0]


def fwd_loss(h, a, units, target, idxs, d):
    rows, f = a.shape
    nu = len(units)
    rb = LROWS if nu == 1 else LROWS // 2
    w = units[0][2][1]
    scale = 2.0 / (rows * d)
    hs = [view(h, (), (rows, w), 0, i) for i in idxs]
    ts = [view(target[0], target[1], (rows, w), 0, i) for i in idxs]
    av = view(a, (), (rows, f))

    def kernel(a_ref, *refs):
        h_refs, t_refs, w_refs, o_refs = refs[:nu], refs[nu:2 * nu], refs[2 * nu:3 * nu], refs[3 * nu:]
        for j in range(nu):
            out = (h_refs[j][...].astype(F32) + nn(a_ref[...], w_refs[j][...].astype(BF))).astype(BF)
            e = scale * (out.astype(F32) - t_refs[j][...].astype(F32))
            o_refs[j][...] = e
            o_refs[nu + j][...] = e.astype(BF)

    ov = view(None, (), (rows, w))
    res = run(kernel, rows // rb, [(av, by_rows(av, rb))] + [(v, by_rows(v, rb)) for v in hs + ts] + [(u, whole(u)) for u in units],
              [(jax.ShapeDtypeStruct((rows, w), dt), by_rows(ov, rb)) for dt in (F32, BF) for _ in units],
              flops=2 * rows * w * nu * f, nbytes=2 * rows * f)
    return res[:nu], res[nu:]


def back_both(errs, twos, slope, ones, h, wide, from_z):
    rows, f = slope.shape
    d = h[2][1]
    ne, nu = len(errs), len(ones)
    per, w = f // nu, d // ne

    def kernel(s_ref, h_ref, *refs):
        e_refs, w2_refs, w1_refs, x_refs = refs[:ne], refs[ne:2 * ne], refs[2 * ne:2 * ne + nu], refs[2 * ne + nu:3 * ne + nu]
        dz_ref, o_ref, m_ref = refs[-3:]
        for c in range(0, f, SUB):
            u = nt(e_refs[0][...], w2_refs[0][c:c + SUB, :].astype(BF))
            for k in range(1, ne):
                u += nt(e_refs[k][...], w2_refs[k][c:c + SUB, :].astype(BF))
            dz_ref[:, c:c + SUB] = (u * (gelu_slope(s_ref[:, c:c + SUB]) if from_z else s_ref[:, c:c + SUB])).astype(BF)
        for c in range(0, d, SUB):
            m = nt(dz_ref[:, :per], w1_refs[0][c:c + SUB, :].astype(BF))
            for j in range(1, nu):
                m += nt(dz_ref[:, j * per:(j + 1) * per], w1_refs[j][c:c + SUB, :].astype(BF))
            m_ref[:, c:c + SUB] = m
        n, inv = norm_of(h_ref[...])
        m = m_ref[...]
        back = inv * (m - n * jnp.mean(m * n, axis=-1, keepdims=True))
        for k in range(ne):
            o_ref[:, k * w:(k + 1) * w] = (x_refs[k][...] + back[:, k * w:(k + 1) * w]).astype(BF)

    sv = view(slope, (), (rows, f))
    ov = view(None, (), (rows, d))
    rb = BROWS
    return run(kernel, rows // rb,
               [(sv, by_rows(sv, rb)), (h, by_rows(h, rb))] + [(view(e, (), e.shape), by_rows(view(e, (), e.shape), rb)) for e in errs]
               + [(u, whole(u)) for u in list(twos) + list(ones)] + [(view(e, (), e.shape), by_rows(view(e, (), e.shape), rb)) for e in wide],
               [(jax.ShapeDtypeStruct((rows, f), BF), by_rows(sv, rb)), (jax.ShapeDtypeStruct((rows, d), BF), by_rows(ov, rb))],
               scratch=[pltpu.VMEM((rb, d), F32)], flops=4 * rows * f * d, nbytes=10 * rows * f)


def grad_cols(errs, a, olds, cuts):
    rows, w = errs[0].shape
    f = a.shape[1]
    nu = len(olds)
    kr = CROWS
    steps = rows // kr
    outs, kinds = [], []
    for j in range(nu):
        outs += [jax.ShapeDtypeStruct((f, w), F32), jax.ShapeDtypeStruct((f, w), BF)] + [jax.ShapeDtypeStruct((f // cuts[j], w), BF)] * (cuts[j] if cuts[j] > 1 else 0)
        kinds += [(j, -2), (j, -1)] + [(j, k) for k in range(cuts[j] if cuts[j] > 1 else 0)]

    def kernel(a_ref, *refs):
        e_refs, p_refs, o_refs, acc_ref = refs[:nu], refs[nu:2 * nu], dict(zip(kinds, refs[2 * nu:-1])), refs[-1]
        i = pl.program_id(0)
        sts = [e_ref[...].T for e_ref in e_refs]

        @pl.when(i == 0)
        def _():
            for j in range(nu):
                for c in range(0, f, SUB):
                    acc_ref[j * w:(j + 1) * w, c:c + SUB] = nn(sts[j], a_ref[:, c:c + SUB])

        @pl.when(i > 0)
        def _():
            for j in range(nu):
                for c in range(0, f, SUB):
                    acc_ref[j * w:(j + 1) * w, c:c + SUB] += nn(sts[j], a_ref[:, c:c + SUB])

        @pl.when(i == steps - 1)
        def _():
            for j in range(nu):
                size = f // cuts[j]
                for c in range(0, f, SUB):
                    q = p_refs[j][c:c + SUB, :] - LEARN_RATE * acc_ref[j * w:(j + 1) * w, c:c + SUB].T
                    low = q.astype(BF)
                    o_refs[j, -2][c:c + SUB, :] = q
                    o_refs[j, -1][c:c + SUB, :] = low
                    if cuts[j] > 1:
                        o_refs[j, c // size][c % size:c % size + SUB, :] = low

    av = view(a, (), (rows, f))
    es = [view(e, (), (rows, w)) for e in errs]
    res = run(kernel, steps, [(av, by_rows(av, kr))] + [(e, by_rows(e, kr)) for e in es] + [(u, whole(u)) for u in olds],
              [(o, pl.BlockSpec(o.shape, lambda i: (0, 0))) for o in outs], scratch=[pltpu.VMEM((nu * w, f), F32)],
              flops=2 * rows * nu * w * f, nbytes=2 * rows * f)
    got = dict(zip(kinds, res))
    return [(got[j, -2], got[j, -1], [got[j, k] for k in range(cuts[j])] if cuts[j] > 1 else [got[j, -1]]) for j in range(nu)]


def back_act(errs, units, slope, from_z, lo=0, of=1):
    rows, f = slope.shape
    f = f // of
    ne, nu = len(errs), len(units)
    rb = MROWS // 2 if from_z and of == 1 else MROWS
    per = units[0][2][0]

    def kernel(*refs):
        e_refs, w_refs = refs[:ne], refs[ne:ne + nu]
        s_ref, o_ref = refs[ne + nu:]
        for c in range(0, f, SUB):
            if ne > 1:
                u = nt(e_refs[0][...], w_refs[0][c:c + SUB, :].astype(BF))
                for k in range(1, ne):
                    u += nt(e_refs[k][...], w_refs[k][c:c + SUB, :].astype(BF))
            else:
                r = c % per
                u = nt(e_refs[0][...], w_refs[c // per][r:r + SUB, :].astype(BF))
            o_ref[:, c:c + SUB] = (u * (gelu_slope(s_ref[:, c:c + SUB]) if from_z else s_ref[:, c:c + SUB])).astype(BF)

    if ne > 1:
        units = [view(arr, lead, (f, shape[1]), lo, cb) for arr, lead, shape, _, cb in units]
    vs = [view(e, (), e.shape) for e in errs]
    sv = view(slope, (), (rows, f), 0, lo)
    ov = view(None, (), (rows, f))
    return run(kernel, rows // rb, [(v, by_rows(v, rb)) for v in vs] + [(u, whole(u)) for u in units] + [(sv, by_rows(sv, rb))],
               [(jax.ShapeDtypeStruct((rows, f), BF), by_rows(ov, rb))], flops=2 * rows * f * 768, nbytes=6 * rows * f)[0]


def back_norm(dzs, units, h, errs):
    rows, fp = dzs[0].shape
    nd = len(dzs)
    f = fp * nd
    d = h[2][1]
    ne, nu = len(errs), len(units)
    per = f // nu

    def kernel(*refs):
        dz_refs, refs = refs[:nd], refs[nd:]
        part = lambda j: dz_refs[j * per // fp][:, j * per % fp:j * per % fp + per]
        w_refs, h_ref, e_refs, o_ref, m_ref = refs[:nu], refs[nu], refs[nu + 1:nu + 1 + ne], refs[-2], refs[-1]
        for c in range(0, d, SUB):
            m = nt(part(0), w_refs[0][c:c + SUB, :].astype(BF))
            for j in range(1, nu):
                m += nt(part(j), w_refs[j][c:c + SUB, :].astype(BF))
            m_ref[:, c:c + SUB] = m
        n, inv = norm_of(h_ref[...])
        m = m_ref[...]
        back = inv * (m - n * jnp.mean(m * n, axis=-1, keepdims=True))
        w = d // ne
        for k in range(ne):
            o_ref[:, k * w:(k + 1) * w] = (e_refs[k][...] + back[:, k * w:(k + 1) * w]).astype(BF)

    dv = view(None, (), (rows, fp))
    vs = [view(e, (), e.shape) for e in errs]
    ov = view(None, (), (rows, d))
    return run(kernel, rows // MROWS,
               [(dz, by_rows(dv, MROWS)) for dz in dzs] + [(u, whole(u)) for u in units] + [(h, by_rows(h, MROWS))] + [(v, by_rows(v, MROWS)) for v in vs],
               [(jax.ShapeDtypeStruct((rows, d), BF), by_rows(ov, MROWS))], scratch=[pltpu.VMEM((MROWS, d), F32)],
               flops=2 * rows * f * d, nbytes=2 * rows * f)[0]


def grad_update(small, big, olds, cuts, use_norm, flip):
    rows, m = small[2]
    n = big[2][1]
    nu = len(olds)
    per = n // nu
    steps = rows // KROWS
    out_shapes, out_kinds = [], []
    for j, u in enumerate(olds):
        r, c = u[2]
        out_shapes += [((r, c), F32), ((r, c), BF)] + ([((r // cuts[j], c), BF)] * cuts[j] if cuts[j] > 1 else [])
        out_kinds += [(j, -2), (j, -1)] + ([(j, k) for k in range(cuts[j])] if cuts[j] > 1 else [])

    def kernel(s_ref, b_ref, *refs):
        p_refs, o_refs, acc_ref = refs[:nu], refs[nu:-1], refs[-1]
        i = pl.program_id(0)
        s = s_ref[...]
        if use_norm:
            s = norm_of(s)[0].astype(BF)
        st = s.T

        @pl.when(i == 0)
        def _():
            for c in range(0, n, SUB):
                acc_ref[:, c:c + SUB] = nn(st, b_ref[:, c:c + SUB])

        @pl.when(i > 0)
        def _():
            for c in range(0, n, SUB):
                acc_ref[:, c:c + SUB] += nn(st, b_ref[:, c:c + SUB])

        @pl.when(i == steps - 1)
        def _():
            for (j, kind), o_ref in zip(out_kinds, o_refs):
                if kind != -2:
                    continue
                w_ref = o_refs[out_kinds.index((j, -1))]
                pieces = [o_refs[out_kinds.index((j, k))] for k in range(cuts[j])] if cuts[j] > 1 else []
                size = olds[j][2][0] // cuts[j]
                for c in range(0, per, SUB):
                    g = acc_ref[:, j * per + c:j * per + c + SUB]
                    at = (slice(c, c + SUB), slice(None)) if flip else (slice(None), slice(c, c + SUB))
                    q = p_refs[j][at] - LEARN_RATE * (g.T if flip else g)
                    low = q.astype(BF)
                    o_ref[at] = q
                    w_ref[at] = low
                    for k, piece in enumerate(pieces):
                        if flip:
                            lo, hi = max(c, k * size), min(c + SUB, (k + 1) * size)
                            if lo < hi:
                                piece[lo - k * size:hi - k * size, :] = low[lo - c:hi - c]
                        else:
                            piece[:, c:c + SUB] = low[k * size:(k + 1) * size]

    res = run(kernel, steps, [(small, by_rows(small, KROWS)), (big, by_rows(big, KROWS))] + [(u, whole(u)) for u in olds],
              [(jax.ShapeDtypeStruct(sh, dt), pl.BlockSpec(sh, lambda i: (0, 0))) for sh, dt in out_shapes],
              scratch=[pltpu.VMEM((m, n), F32)], flops=2 * rows * m * n, nbytes=10 * m * n)
    got = {kind: r for kind, r in zip(out_kinds, res)}
    return [(got[j, -2], got[j, -1], [got[j, k] for k in range(cuts[j])] if cuts[j] > 1 else [got[j, -1]]) for j in range(nu)]


COMB_ROWS = {768: 384, 256: 1536}


def combine(even, own, cc, xx, yy, final):
    rows, cols = own.shape
    nc = len(xx)
    blk = rows // nc if nc > 1 else COMB_ROWS[cols]

    def kernel(even_ref, q_ref, c_ref, *refs):
        def mix(x, y):
            prev = jnp.where(even_ref[0] == 1, y, x).astype(F32)
            nxt = jnp.where(even_ref[0] == 1, x, y).astype(F32)
            c = c_ref[...].astype(F32)
            p = (q_ref[...] + c + c + prev + nxt) / 5.0
            if final is None:
                refs[2 * nc][...] = p
                refs[2 * nc + 1][...] = p.astype(BF)
            else:
                refs[-1][...] = p

        if nc == 1:
            mix(refs[0][...], refs[1][...])
        else:
            for k in range(nc):
                @pl.when(pl.program_id(0) == k)
                def _(k=k):
                    mix(refs[k][...], refs[nc + k][...])

    ov = view(None, (), (rows, cols))
    spec = by_rows(ov, blk)
    pv = view(None, (), (rows // nc, cols))
    piece = by_rows(pv, blk) if nc == 1 else whole(pv)
    ins = [(even, pl.BlockSpec(memory_space=pltpu.SMEM)), (own, spec), (cc, spec)] + [(v, piece) for v in list(xx) + list(yy)]
    if final is None:
        return run(kernel, rows // blk, ins, [(jax.ShapeDtypeStruct((rows, cols), F32), spec), (jax.ShapeDtypeStruct((rows, cols), BF), spec)],
                   nbytes=18 * rows * cols, flops=8 * rows * cols)
    arr, shape, layer, rb, cb = final
    aliases = None
    if arr is not None:
        aliases = {len(ins): 0}
        ins.append((arr, ANY))
    fv = (None, (0, 0, layer), (rows, cols), rb, cb)
    return run(kernel, rows // blk, ins, [(jax.ShapeDtypeStruct(shape, F32), by_rows(fv, blk))], aliases, nbytes=14 * rows * cols, flops=8 * rows * cols)


X_SWAP, Y_SWAP = [[(r, r ^ bit) for r in range(4)] for bit in (1, 2)]
C_SWAP = [(c, 1 - c) for c in range(2)]

L1B = ["A", "B", "C"]
ONE0, TWO0, ONE1 = [[f"{k}{j}" for j in range(4)] for k in "abd"]
UNITS = L1B + ONE0 + TWO0 + ONE1
KINDS = "comb f1 f2 fl".split() + "gl g1 g2 u".split() + ["m", "v"]
PLAN = [
    {
        "wires": (11121006090403, 7080513140102), "halved": 25278,
        "f1": ((4,), (4,)), "g1": ((2, 2), (2, 2)), "g2": (1, 1, 1, 1),
        "fl": (123,), "gl": (1, 23), "u0": 1, "u1": 1, "z": (1, 1),
    },
    {
        "wires": (12110708040305, 10060913140201), "halved": 12782,
        "f1": ((2, 2), (2, 2)), "g1": ((2, 1, 1), (2, 2)), "g2": (2, 2),
        "fl": (1, 2, 3), "gl": (1, 23), "u0": 1, "u1": 2, "z": (0, 0),
    },
    {
        "wires": (2011411081007, 5130406030912), "halved": 26716,
        "f1": ((2, 1, 1), (2, 1, 1)), "g1": ((2, 2), (1, 1, 1, 1)), "g2": (2, 1, 1),
        "fl": (1, 2, 3), "gl": (1, 2, 3), "u0": 2, "u1": 1, "z": (0, 0),
    },
]

LAST = 3
CALLS = [
    100000002000000010100000, 300000004000000070100011, 501000008000102260030000, 700010115001100000110011,
    600210005000002150111042, 600010000010102140011000, 600120000000211600031000, 600000009000000071000,
    1210000004000011000000, 820000005100011011000, 210010001110100000141000, 1300001111000031001000,
    410010000001001131010000, 200003102000071100000, 511010007111003281001000, 610010007100104201001000,
    510010005111103201121000, 11100005101100051021021, 610100000108307541010000, 10410420107100001030000,
    120010000110000001050000, 120110000106000012021000, 10910002200000012101000, 11300001211100001140000,
    121210003200000042001000, 10210113202000042020000, 10100213201100042010000, 920010115213100052101021,
    720010216200100052121011, 720110006202000062011022, 20100005201000002021032, 520000005211107402111011,
    21400000200100002080000, 20510000207100002043000, 21310000210000002061000, 20920000203000002120000,
]
N_STEPS = len(PLAN)


def spans(sizes):
    return [tuple(range(sum(sizes[:k]), sum(sizes[:k + 1]))) for k in range(len(sizes))]


for _cfg in PLAN:
    _digits = "".join(str(n).zfill(size) for n, size in zip(_cfg["wires"], (16, 14)))
    _cfg["wires"] = [UNITS[int(_digits[i:i + 2])] for i in range(0, len(_digits), 2)]
    _cfg["halved"] = [u for i, u in enumerate(UNITS) if _cfg["halved"] >> i & 1]
    for _key in ("fl", "gl"):
        _cfg[_key] = [[L1B[int(i) - 1] for i in str(group)] for group in _cfg[_key]]
    _cfg["f1"], _cfg["g1"] = [[spans(v) for v in _cfg[_key]] for _key in ("f1", "g1")]
    _cfg["g2"] = spans(_cfg["g2"])


def halves(t, u):
    return 2 if u in PLAN[t]["halved"] else 1


def issue_order():
    units = [(t, u) for t in range(N_STEPS) for u in PLAN[t]["wires"]]
    both = [f"{t}_{u}_{k}" for t, u in units for k in range(halves(t, u))]
    queue = {"y": iter(both), "x": iter(both), "c": iter([f"{t}_{u}" for t, u in units])}
    order = []
    digits = "".join(str(n).zfill(24) for n in CALLS[:-1]) + str(CALLS[-1]).zfill(8 * LAST)
    for i in range(0, len(digits), 8):
        code = digits[i:i + 8]
        kind, t, arg = KINDS[int(code[0])], code[1], code[2:4]
        for link, count in (("y", code[4]), ("x", code[5:7]), ("c", code[7])):
            order += [link + next(queue[link]) for _ in range(int(count))]
        if kind == "comb":
            arg = UNITS[int(arg)]
        elif kind not in ("f1", "g1", "g2", "u"):
            arg = str(int(arg))
        order.append(f"{kind}{t}_{arg}")
    return order


ORDER = issue_order()


def solution(mesh):
    def device_fn(w_one, w_two, inputs, targets):
        _, d, f = w_one.shape[2:]
        rows = inputs.shape[3]
        quarter, third = f // 4, d // 3
        even = (1 - lax.rem(lax.axis_index("row"), 2)).astype(jnp.int32).reshape((1,))
        names = {0: ONE0, 1: ONE1}
        master, where = {}, {}
        for j in range(4):
            for lay in (0, 1):
                where[names[lay][j]] = ("one", lay, (d, quarter), 0, j)
            where[TWO0[j]] = ("two", 0, (quarter, d), j, 0)
        for j, u in enumerate(L1B):
            where[u] = ("two", 1, (f, third), 0, j)
        src = {"one": w_one, "two": w_two}
        for u, (which, lay, shape, rb, cb) in where.items():
            master[u] = view(src[which], (0, 0, lay), shape, rb, cb)
        low = dict(master)
        final = {"one": None, "two": None}
        st, own, wire, cut, moved = {}, {}, {}, {}, {}

        def keep(t, units, got):
            for u, (q, b, parts) in zip(units, got):
                own[t, u], wire[t, u], cut[t, u] = q, b, parts

        def issue(name):
            part = name.split("_")
            t, kind, rest = int(part[0][-1]), part[0][:-1], part[1]
            cfg = PLAN[t]
            x_in = view(inputs, (0, 0, t), (rows, d))
            hidden = lambda lay: x_in if lay == 0 else view(st["h", t], (), (rows, d))
            lows = lambda us: [low[u] for u in us]
            if kind == "x":
                moved[name] = lax.ppermute(cut[t, rest][int(part[2])], "row", X_SWAP)
            elif kind == "y":
                moved[name] = lax.ppermute(moved["x" + name[1:]], "row", Y_SWAP)
            elif kind == "c":
                moved[name] = lax.ppermute(wire[t, rest], "col", C_SWAP)
            elif kind == "comb":
                xx, yy = [[moved[f"{r}{t}_{rest}_{k}"] for k in range(halves(t, rest))] for r in "xy"]
                args = (even, own[t, rest], moved[f"c{t}_{rest}"], xx, yy)
                if t == N_STEPS - 1:
                    which, lay, _, rb, cb = where[rest]
                    final[which] = combine(*args, (final[which], src[which].shape, lay, rb, cb))[0]
                else:
                    p, b = combine(*args, None)
                    master[rest], low[rest] = view(p, (), p.shape), view(b, (), b.shape)
            elif kind == "f1":
                lay, g = int(rest[0]), int(rest[1])
                idx = cfg["f1"][lay][g]
                prev = (st["a", t, lay], st["s", t, lay]) if g else None
                st["a", t, lay], st["s", t, lay] = fwd_one(hidden(lay), lows(names[lay][j] for j in idx), prev, idx[0], cfg["z"][lay])
            elif kind == "f2":
                st["h", t] = fwd_two(x_in, st["a", t, 0], lows(TWO0))
            elif kind == "fl":
                us = cfg["fl"][int(rest)]
                target = view(targets, (0, 0, t), (rows, d))
                wide, eb = fwd_loss(st["h", t], st["a", t, 1], lows(us), target, [L1B.index(u) for u in us], d)
                for k, u in enumerate(us):
                    st["e", t, u], st["eb", t, u] = wide[k], eb[k]
            elif kind == "v":
                st["dz", t, 1, 0], st["e0", t] = back_both([st["eb", t, u] for u in L1B], lows(L1B), st["s", t, 1], lows(ONE1), hidden(1), [st["e", t, u] for u in L1B], cfg["z"][1])
            elif kind == "u" and rest[0] == "1":
                g, of = int(rest[1]), cfg["u1"]
                st["dz", t, 1, g] = back_act([st["eb", t, u] for u in L1B], lows(L1B), st["s", t, 1], cfg["z"][1], g, of)
            elif kind == "m":
                st["e0", t] = back_norm([st["dz", t, 1, g] for g in range(cfg["u1"])], lows(ONE1), hidden(1), [st["e", t, u] for u in L1B])
            elif kind == "u":
                g, of = int(rest[1]), cfg["u0"]
                st["dz", t, 0, g] = back_act([st["e0", t]], lows(TWO0[4 // of * g:4 // of * (g + 1)]), st["s", t, 0], cfg["z"][0], g, of)
            elif kind == "gl":
                us = cfg["gl"][int(rest)]
                keep(t, us, grad_cols([st["eb", t, u] for u in us], st["a", t, 1], [master[u] for u in us], [halves(t, u) for u in us]))
            else:
                lay, g = int(rest[0]), int(rest[1])
                idx = cfg["g1"][lay][g] if kind == "g1" else cfg["g2"][g]
                us = [(names[lay] if kind == "g1" else TWO0)[j] for j in idx]
                n = len(idx)
                if kind == "g2":
                    small, big = view(st["e0", t], (), (rows, d)), view(st["a", t, 0], (), (rows, n * quarter), 0, idx[0] // n)
                else:
                    per = 4 // cfg["u1" if lay else "u0"]
                    small, big = hidden(lay), view(st["dz", t, lay, idx[0] // per], (), (rows, n * quarter), 0, (idx[0] % per) // n)
                keep(t, us, grad_update(small, big, [master[u] for u in us], [halves(t, u) for u in us], kind == "g1", kind == "g2"))

        for name in ORDER:
            issue(name)
        return final["one"], final["two"]

    spec = P("row", "col")
    return jax.shard_map(device_fn, mesh=mesh, in_specs=(spec,) * 4, out_specs=(spec, spec), check_vma=False)
```

time: 2570 us -> 2390 us (0.930)
  waiting for transfers between devices: 1320 us -> 1180 us
  Pallas kernels: 1100 us -> 1050 us
    ppermute x45 -> x70, waiting for transfers between devices: 677 us -> 508 us  [issue(): moved[name] = lax.ppermute(cut[t, rest][int(part[2])], 'row', X_SWAP)]
    pallas_call x111 -> x108, Pallas kernels: 1100 us -> 1050 us  [run(): pl.pallas_call(kernel, grid=(grid,), in_specs=[spec for _, spec in ins],...]
    ppermute x45 -> x70, waiting for transfers between devices: 639 us -> 672 us  [issue(): moved[name] = lax.ppermute(moved['x' + name[1:]], 'row', Y_SWAP)]
    ppermute x45 -> x70, starting transfers between devices: 51.6 us -> 75.5 us  [issue(): moved[name] = lax.ppermute(moved['x' + name[1:]], 'row', Y_SWAP)]
    ppermute x45 -> x70, starting transfers between devices: 82.8 us -> 68.8 us  [issue(): moved[name] = lax.ppermute(cut[t, rest][int(part[2])], 'row', X_SWAP)]
  transfers between devices with their start and end apart: 135 -> 185, of which waited for: 66 -> 88; matrix products, arithmetic and copies ran while one was open for 0% -> 0% of each run, Pallas kernels for 31% -> 38%
where the time goes in v3:
time: 2390 us; the launch traced here: 2380 us
  waiting for transfers between devices  1180 us (49%)
  Pallas kernels  1050 us (44%)
  starting transfers between devices  149 us (6%)
    pallas_call x108, Pallas kernels, run(): pl.pallas_call(kernel, grid=(grid,), in_specs=[spec for _, spec in ins],...  1050 us
    ppermute x70, waiting for transfers between devices, issue(): moved[name] = lax.ppermute(moved['x' + name[1:]], 'row', Y_SWAP)  672 us
    ppermute x70, waiting for transfers between devices, issue(): moved[name] = lax.ppermute(cut[t, rest][int(part[2])], 'row', X_SWAP)  508 us
    ppermute x70, starting transfers between devices, issue(): moved[name] = lax.ppermute(moved['x' + name[1:]], 'row', Y_SWAP)  75.5 us
    ppermute x70, starting transfers between devices, issue(): moved[name] = lax.ppermute(cut[t, rest][int(part[2])], 'row', X_SWAP)  68.8 us
  transfers between devices with their start and end apart: 185, of which 88 were waited for; matrix products, arithmetic and copies ran while one was open for 0% of the time, Pallas kernels for 38%

profile of v3, /device:TPU:0, one launch (start us, length us, event | category | flops | bytes accessed | tf_op | source)
XLA Modules:
  0.0 2384.8 jit_solution(5977362813706860614)
XLA Ops:
  0.6 20.5 shard_map.59
  21.1 16.3 shard_map.60.h_ref.refs_0_.refs_1_.refs_2_.refs_5_.s_ref
  37.5 20.5 shard_map.61
  58.0 17.9 shard_map.62
  75.9 26.2 %shard_map.63.refs_0_.b_ref = bf16[2048,3072]{1,0:T(8,128)(2,1)} custom-call(bf16[2048,256]{1,0:T(8,128)(2,1)} %get-tuple-element.248.refs_0_, bf16[2048,256]{1,0:T(8,128)(2,1)} %get-tuple-element.249.refs_1_.refs_0_, bf16[2048,256]{1,0:T(8,128)(2,1)} %get-tuple-element.250.refs_2_.refs_1_, f32[1,1,2,3072,768]{4,3,2,1,0:T(8,128)} %refs_3_.15, ...), custom_call_target="tpu_custom_call" | custom-call | flops 9663676416 | bytes 37748736 | tf_op jit(solution)/shard_map/pallas_call | solution.py:60
  102.1 18.9 shard_map.64.refs_0_.s_ref
  162.6 25.9 %shard_map.65.b_ref = bf16[2048,3072]{1,0:T(8,128)(2,1)} custom-call(bf16[2048,768]{1,0:T(8,128)(2,1)} %shard_map.64.refs_0_.s_ref, f32[1,1,2,3072,768]{4,3,2,1,0:T(8,128)} %refs_3_.15, f32[1,1,2,3072,768]{4,3,2,1,0:T(8,128)} %refs_3_.15, f32[1,1,2,3072,768]{4,3,2,1,0:T(8,128)} %refs_3_.15, f32[1,1,2,3072,768]{4,3,2,1,0:T(8,128)} %refs_3_.15, ...), custom_call_target="tpu_custom_call" | custom-call | flops 9663676416 | bytes 37748736 | tf_op jit(solution)/shard_map/pallas_call | solution.py:60
  257.6 18.4 shard_map.94
  320.8 16.7 collective-permute-done.54.refs_0_
  354.4 16.8 collective-permute-done.59.refs_0_
  371.2 42.2 %collective-permute-done.60.refs_1_ = bf16[1536,256]{1,0:T(8,128)(2,1)} collective-permute-done((bf16[1536,256]{1,0:T(8,128)(2,1)}, bf16[1536,256]{1,0:T(8,128)(2,1)}, u32[]{:S(2)}, u32[]{:S(2)}) %collective-permute-start.60) | collective-permute-done | bytes 786464 | tf_op jit(solution)/shard_map/ppermute | solution.py:529
  415.5 20.7 collective-permute-done.24.refs_0_
  608.9 15.7 collective-permute-done.56.refs_2_
  626.1 15.4 collective-permute-done.57.refs_3_
  643.0 15.4 collective-permute-done.61.refs_2_
  672.1 28.3 %collective-permute-done.62.refs_3_ = bf16[1536,256]{1,0:T(8,128)(2,1)S(1)} collective-permute-done((bf16[1536,256]{1,0:T(8,128)(2,1)}, bf16[1536,256]{1,0:T(8,128)(2,1)S(1)}, u32[]{:S(2)}, u32[]{:S(2)}) %collective-permute-start.62) | collective-permute-done | bytes 786464 | tf_op jit(solution)/shard_map/ppermute | solution.py:531
  704.9 21.0 collective-permute-done.25.refs_1_
  816.6 14.9 shard_map.82.h_ref.refs_0_.refs_6_.s_ref
  880.9 18.6 shard_map.132
  956.2 17.7 shard_map.101.refs_0_.s_ref
  973.8 19.3 shard_map.102.b_ref
  1192.6 15.6 collective-permute-done.124.refs_2_
  1209.5 15.6 collective-permute-done.125.refs_3_
  1435.1 25.3 %collective-permute-done.80.refs_1_ = bf16[768,768]{1,0:T(8,128)(2,1)} collective-permute-done((bf16[768,768]{1,0:T(8,128)(2,1)}, bf16[768,768]{1,0:T(8,128)(2,1)}, u32[]{:S(2)}, u32[]{:S(2)}) %collective-permute-start.80) | collective-permute-done | bytes 1179680 | tf_op jit(solution)/shard_map/ppermute | solution.py:531
  1652.1 30.3 %shard_map.137 = (bf16[2048,3072]{1,0:T(8,128)(2,1)}, bf16[2048,768]{1,0:T(8,128)(2,1)}) custom-call(f32[2048,3072]{1,0:T(8,128)} %get-tuple-element.404.s_ref, bf16[2048,768]{1,0:T(8,128)(2,1)} %shard_map.119.h_ref.refs_0_.s_ref, bf16[2048,256]{1,0:T(8,128)(2,1)} %get-tuple-element.410.refs_0_, bf16[2048,256]{1,0:T(8,128)(2,1)} %get-tuple-element.418.refs_1_.refs_0_, ...), custom_call_target="tpu_custom_call" | custom-call | flops 19327352832 | bytes 62914560 | tf_op jit(solution)/shard_map/pallas_call | solution.py:60
  1956.8 23.6 collective-permute-done.172.refs_0_
  1981.3 24.3 %collective-permute-done.166.refs_0_ = bf16[768,768]{1,0:T(8,128)(2,1)S(1)} collective-permute-done((bf16[768,768]{1,0:T(8,128)(2,1)}, bf16[768,768]{1,0:T(8,128)(2,1)S(1)}, u32[]{:S(2)}, u32[]{:S(2)}) %collective-permute-start.166) | collective-permute-done | bytes 1179680 | tf_op jit(solution)/shard_map/ppermute | solution.py:529
  2006.4 22.5 collective-permute-done.127.refs_0_
  2170.7 19.3 collective-permute-done.150.refs_0_
  2196.5 58.2 %collective-permute-done.173.refs_1_ = bf16[768,768]{1,0:T(8,128)(2,1)S(1)} collective-permute-done((bf16[768,768]{1,0:T(8,128)(2,1)}, bf16[768,768]{1,0:T(8,128)(2,1)S(1)}, u32[]{:S(2)}, u32[]{:S(2)}) %collective-permute-start.173) | collective-permute-done | bytes 1179680 | tf_op jit(solution)/shard_map/ppermute | solution.py:531
  2254.7 25.3 %collective-permute-done.128.refs_1_ = bf16[768,768]{1,0:T(8,128)(2,1)S(1)} collective-permute-done((bf16[768,768]{1,0:T(8,128)(2,1)}, bf16[768,768]{1,0:T(8,128)(2,1)S(1)}, u32[]{:S(2)}, u32[]{:S(2)}) %collective-permute-start.128) | collective-permute-done | bytes 1179680 | tf_op jit(solution)/shard_map/ppermute | solution.py:531
  2280.8 24.5 %collective-permute-done.151.refs_1_ = bf16[768,768]{1,0:T(8,128)(2,1)S(1)} collective-permute-done((bf16[768,768]{1,0:T(8,128)(2,1)S(1)}, bf16[768,768]{1,0:T(8,128)(2,1)S(1)}, u32[]{:S(2)}, u32[]{:S(2)}) %collective-permute-start.151) | collective-permute-done | bytes 1179680 | tf_op jit(solution)/shard_map/ppermute | solution.py:531
  (624 shorter events, 1671.4 us)
Async XLA Ops:
  308.1 106.9 %collective-permute-start.32 = (bf16[768,768]{1,0:T(8,128)(2,1)}, bf16[768,768]{1,0:T(8,128)(2,1)}, u32[]{:S(2)}, u32[]{:S(2)}) collective-permute-start(bf16[768,768]{1,0:T(8,128)(2,1)} %get-tuple-element.291), channel_id=1, source_target_pairs={{0,2},{2,0},{4,6},{6,4},{1,3},{3,1},{5,7},{7,5}} | collective-permute-start | bytes 3538952 | tf_op jit(solution)/shard_map/ppermute | solution.py:529
  320.8 94.2 %collective-permute-start.31 = (bf16[768,768]{1,0:T(8,128)(2,1)}, bf16[768,768]{1,0:T(8,128)(2,1)S(1)}, u32[]{:S(2)}, u32[]{:S(2)}) collective-permute-start(bf16[768,768]{1,0:T(8,128)(2,1)} %get-tuple-element.291), channel_id=1, source_target_pairs={{0,1},{1,0},{2,3},{3,2},{4,5},{5,4},{6,7},{7,6}} | collective-permute-start | bytes 3538952 | tf_op jit(solution)/shard_map/ppermute | solution.py:533
  354.4 81.9 %collective-permute-start.24 = (bf16[768,768]{1,0:T(8,128)(2,1)}, bf16[768,768]{1,0:T(8,128)(2,1)}, u32[]{:S(2)}, u32[]{:S(2)}) collective-permute-start(bf16[768,768]{1,0:T(8,128)(2,1)} %get-tuple-element.283), channel_id=1, source_target_pairs={{0,2},{2,0},{4,6},{6,4},{1,3},{3,1},{5,7},{7,5}} | collective-permute-start | bytes 3538952 | tf_op jit(solution)/shard_map/ppermute | solution.py:529
  607.6 94.1 %collective-permute-start.53 = (bf16[3072,256]{1,0:T(8,128)(2,1)}, bf16[3072,256]{1,0:T(8,128)(2,1)}, u32[]{:S(2)}, u32[]{:S(2)}) collective-permute-start(bf16[3072,256]{1,0:T(8,128)(2,1)} %get-tuple-element.317), channel_id=1, source_target_pairs={{0,1},{1,0},{2,3},{3,2},{4,5},{5,4},{6,7},{7,6}} | collective-permute-start | bytes 4718600 | tf_op jit(solution)/shard_map/ppermute | solution.py:533
  607.6 95.8 %collective-permute-start.58 = (bf16[3072,256]{1,0:T(8,128)(2,1)}, bf16[3072,256]{1,0:T(8,128)(2,1)S(1)}, u32[]{:S(2)}, u32[]{:S(2)}) collective-permute-start(bf16[3072,256]{1,0:T(8,128)(2,1)} %get-tuple-element.323), channel_id=1, source_target_pairs={{0,1},{1,0},{2,3},{3,2},{4,5},{5,4},{6,7},{7,6}} | collective-permute-start | bytes 4718600 | tf_op jit(solution)/shard_map/ppermute | solution.py:533
  701.4 95.3 %collective-permute-start.51 = (bf16[3072,256]{1,0:T(8,128)(2,1)}, bf16[3072,256]{1,0:T(8,128)(2,1)S(1)}, u32[]{:S(2)}, u32[]{:S(2)}) collective-permute-start(bf16[3072,256]{1,0:T(8,128)(2,1)} %get-tuple-element.313), channel_id=1, source_target_pairs={{0,2},{2,0},{4,6},{6,4},{1,3},{3,1},{5,7},{7,5}} | collective-permute-start | bytes 4718600 | tf_op jit(solution)/shard_map/ppermute | solution.py:529
  701.7 89.7 %collective-permute-start.46 = (bf16[768,768]{1,0:T(8,128)(2,1)}, bf16[768,768]{1,0:T(8,128)(2,1)}, u32[]{:S(2)}, u32[]{:S(2)}) collective-permute-start(bf16[768,768]{1,0:T(8,128)(2,1)} %copy-done.20), channel_id=1, source_target_pairs={{0,4},{2,6},{4,0},{6,2},{1,5},{3,7},{5,1},{7,3}} | collective-permute-start | bytes 3538952 | tf_op jit(solution)/shard_map/ppermute | solution.py:531
  703.4 92.2 %collective-permute-start.48 = (bf16[768,768]{1,0:T(8,128)(2,1)}, bf16[768,768]{1,0:T(8,128)(2,1)}, u32[]{:S(2)}, u32[]{:S(2)}) collective-permute-start(bf16[768,768]{1,0:T(8,128)(2,1)} %get-tuple-element.307), channel_id=1, source_target_pairs={{0,2},{2,0},{4,6},{6,4},{1,3},{3,1},{5,7},{7,5}} | collective-permute-start | bytes 3538952 | tf_op jit(solution)/shard_map/ppermute | solution.py:529
  704.9 91.3 %collective-permute-start.5 = (bf16[768,768]{1,0:T(8,128)(2,1)}, bf16[768,768]{1,0:T(8,128)(2,1)}, u32[]{:S(2)}, u32[]{:S(2)}) collective-permute-start(bf16[768,768]{1,0:T(8,128)(2,1)} %get-tuple-element.262), channel_id=1, source_target_pairs={{0,1},{1,0},{2,3},{3,2},{4,5},{5,4},{6,7},{7,6}} | collective-permute-start | bytes 3538952 | tf_op jit(solution)/shard_map/ppermute | solution.py:533
  791.4 110.8 %collective-permute-start.50 = (bf16[3072,256]{1,0:T(8,128)(2,1)}, bf16[3072,256]{1,0:T(8,128)(2,1)S(1)}, u32[]{:S(2)}, u32[]{:S(2)}) collective-permute-start(bf16[3072,256]{1,0:T(8,128)(2,1)} %get-tuple-element.313), channel_id=1, source_target_pairs={{0,1},{1,0},{2,3},{3,2},{4,5},{5,4},{6,7},{7,6}} | collective-permute-start | bytes 4718600 | tf_op jit(solution)/shard_map/ppermute | solution.py:533
  796.7 106.9 %collective-permute-start.52 = (bf16[3072,256]{1,0:T(8,128)(2,1)S(1)}, bf16[3072,256]{1,0:T(8,128)(2,1)}, u32[]{:S(2)}, u32[]{:S(2)}) collective-permute-start(bf16[3072,256]{1,0:T(8,128)(2,1)S(1)} %collective-permute-done.51.refs_0_), channel_id=1, source_target_pairs={{0,4},{2,6},{4,0},{6,2},{1,5},{3,7},{5,1},{7,3}} | collective-permute-start | bytes 4718600 | tf_op jit(solution)/shard_map/ppermute | solution.py:531
  899.6 117.6 %collective-permute-start.117 = (bf16[1536,256]{1,0:T(8,128)(2,1)}, bf16[1536,256]{1,0:T(8,128)(2,1)}, u32[]{:S(2)}, u32[]{:S(2)}) collective-permute-start(bf16[1536,256]{1,0:T(8,128)(2,1)} %get-tuple-element.415), channel_id=1, source_target_pairs={{0,2},{2,0},{4,6},{6,4},{1,3},{3,1},{5,7},{7,5}} | collective-permute-start | bytes 2359304 | tf_op jit(solution)/shard_map/ppermute | solution.py:529
  900.2 117.9 %collective-permute-start.118 = (bf16[1536,256]{1,0:T(8,128)(2,1)}, bf16[1536,256]{1,0:T(8,128)(2,1)}, u32[]{:S(2)}, u32[]{:S(2)}) collective-permute-start(bf16[1536,256]{1,0:T(8,128)(2,1)} %get-tuple-element.416), channel_id=1, source_target_pairs={{0,2},{2,0},{4,6},{6,4},{1,3},{3,1},{5,7},{7,5}} | collective-permute-start | bytes 2359304 | tf_op jit(solution)/shard_map/ppermute | solution.py:529
  901.6 117.6 %collective-permute-start.122 = (bf16[1536,256]{1,0:T(8,128)(2,1)}, bf16[1536,256]{1,0:T(8,128)(2,1)}, u32[]{:S(2)}, u32[]{:S(2)}) collective-permute-start(bf16[1536,256]{1,0:T(8,128)(2,1)} %get-tuple-element.421), channel_id=1, source_target_pairs={{0,2},{2,0},{4,6},{6,4},{1,3},{3,1},{5,7},{7,5}} | collective-permute-start | bytes 2359304 | tf_op jit(solution)/shard_map/ppermute | solution.py:529
  902.2 117.9 %collective-permute-start.123 = (bf16[1536,256]{1,0:T(8,128)(2,1)}, bf16[1536,256]{1,0:T(8,128)(2,1)}, u32[]{:S(2)}, u32[]{:S(2)}) collective-permute-start(bf16[1536,256]{1,0:T(8,128)(2,1)} %get-tuple-element.422), channel_id=1, source_target_pairs={{0,2},{2,0},{4,6},{6,4},{1,3},{3,1},{5,7},{7,5}} | collective-permute-start | bytes 2359304 | tf_op jit(solution)/shard_map/ppermute | solution.py:529
  955.0 80.8 %collective-permute-start.101 = (bf16[384,768]{1,0:T(8,128)(2,1)}, bf16[384,768]{1,0:T(8,128)(2,1)S(1)}, u32[]{:S(2)}, u32[]{:S(2)}) collective-permute-start(bf16[384,768]{1,0:T(8,128)(2,1)} %get-tuple-element.387), channel_id=1, source_target_pairs={{0,2},{2,0},{4,6},{6,4},{1,3},{3,1},{5,7},{7,5}} | collective-permute-start | bytes 1769480 | tf_op jit(solution)/shard_map/ppermute | solution.py:529
  1408.0 103.4 %collective-permute-start.93 = (bf16[768,768]{1,0:T(8,128)(2,1)S(1)}, bf16[768,768]{1,0:T(8,128)(2,1)}, u32[]{:S(2)}, u32[]{:S(2)}) collective-permute-start(bf16[768,768]{1,0:T(8,128)(2,1)S(1)} %collective-permute-done.92.refs_0_), channel_id=1, source_target_pairs={{0,4},{2,6},{4,0},{6,2},{1,5},{3,7},{5,1},{7,3}} | collective-permute-start | bytes 3538952 | tf_op jit(solution)/shard_map/ppermute | solution.py:531
  1421.6 127.1 %collective-permute-start.114 = (bf16[3072,256]{1,0:T(8,128)(2,1)}, bf16[3072,256]{1,0:T(8,128)(2,1)S(1)}, u32[]{:S(2)}, u32[]{:S(2)}) collective-permute-start(bf16[3072,256]{1,0:T(8,128)(2,1)} %get-tuple-element.408), channel_id=1, source_target_pairs={{0,2},{2,0},{4,6},{6,4},{1,3},{3,1},{5,7},{7,5}} | collective-permute-start | bytes 4718600 | tf_op jit(solution)/shard_map/ppermute | solution.py:529
  1434.7 112.6 %collective-permute-start.98 = (bf16[768,768]{1,0:T(8,128)(2,1)}, bf16[768,768]{1,0:T(8,128)(2,1)}, u32[]{:S(2)}, u32[]{:S(2)}) collective-permute-start(bf16[768,768]{1,0:T(8,128)(2,1)} %get-tuple-element.383), channel_id=1, source_target_pairs={{0,2},{2,0},{4,6},{6,4},{1,3},{3,1},{5,7},{7,5}} | collective-permute-start | bytes 3538952 | tf_op jit(solution)/shard_map/ppermute | solution.py:529
  1435.1 112.7 %collective-permute-start.94 = (bf16[768,768]{1,0:T(8,128)(2,1)}, bf16[768,768]{1,0:T(8,128)(2,1)}, u32[]{:S(2)}, u32[]{:S(2)}) collective-permute-start(bf16[768,768]{1,0:T(8,128)(2,1)} %get-tuple-element.378), channel_id=1, source_target_pairs={{0,1},{1,0},{2,3},{3,2},{4,5},{5,4},{6,7},{7,6}} | collective-permute-start | bytes 3538952 | tf_op jit(solution)/shard_map/ppermute | solution.py:533
  1460.4 89.5 %collective-permute-start.96 = (bf16[768,768]{1,0:T(8,128)(2,1)}, bf16[768,768]{1,0:T(8,128)(2,1)}, u32[]{:S(2)}, u32[]{:S(2)}) collective-permute-start(bf16[768,768]{1,0:T(8,128)(2,1)} %collective-permute-done.95.refs_0_), channel_id=1, source_target_pairs={{0,4},{2,6},{4,0},{6,2},{1,5},{3,7},{5,1},{7,3}} | collective-permute-start | bytes 3538952 | tf_op jit(solution)/shard_map/ppermute | solution.py:531
  1511.4 125.6 %collective-permute-start.113 = (bf16[3072,256]{1,0:T(8,128)(2,1)}, bf16[3072,256]{1,0:T(8,128)(2,1)S(1)}, u32[]{:S(2)}, u32[]{:S(2)}) collective-permute-start(bf16[3072,256]{1,0:T(8,128)(2,1)} %get-tuple-element.408), channel_id=1, source_target_pairs={{0,1},{1,0},{2,3},{3,2},{4,5},{5,4},{6,7},{7,6}} | collective-permute-start | bytes 4718600 | tf_op jit(solution)/shard_map/ppermute | solution.py:533
  1548.7 88.4 %collective-permute-start.115 = (bf16[3072,256]{1,0:T(8,128)(2,1)S(1)}, bf16[3072,256]{1,0:T(8,128)(2,1)}, u32[]{:S(2)}, u32[]{:S(2)}) collective-permute-start(bf16[3072,256]{1,0:T(8,128)(2,1)S(1)} %collective-permute-done.114.refs_0_), channel_id=1, source_target_pairs={{0,4},{2,6},{4,0},{6,2},{1,5},{3,7},{5,1},{7,3}} | collective-permute-start | bytes 4718600 | tf_op jit(solution)/shard_map/ppermute | solution.py:531
  1626.5 116.7 %collective-permute-start.178 = (bf16[1536,256]{1,0:T(8,128)(2,1)}, bf16[1536,256]{1,0:T(8,128)(2,1)S(1)}, u32[]{:S(2)}, u32[]{:S(2)}) collective-permute-start(bf16[1536,256]{1,0:T(8,128)(2,1)} %get-tuple-element.485), channel_id=1, source_target_pairs={{0,2},{2,0},{4,6},{6,4},{1,3},{3,1},{5,7},{7,5}} | collective-permute-start | bytes 2359304 | tf_op jit(solution)/shard_map/ppermute | solution.py:529
  1628.2 125.5 %collective-permute-start.179 = (bf16[1536,256]{1,0:T(8,128)(2,1)}, bf16[1536,256]{1,0:T(8,128)(2,1)}, u32[]{:S(2)}, u32[]{:S(2)}) collective-permute-start(bf16[1536,256]{1,0:T(8,128)(2,1)} %get-tuple-element.486), channel_id=1, source_target_pairs={{0,2},{2,0},{4,6},{6,4},{1,3},{3,1},{5,7},{7,5}} | collective-permute-start | bytes 2359304 | tf_op jit(solution)/shard_map/ppermute | solution.py:529
  1807.6 89.1 %collective-permute-start.177 = (bf16[3072,256]{1,0:T(8,128)(2,1)}, bf16[3072,256]{1,0:T(8,128)(2,1)S(1)}, u32[]{:S(2)}, u32[]{:S(2)}) collective-permute-start(bf16[3072,256]{1,0:T(8,128)(2,1)} %get-tuple-element.484), channel_id=1, source_target_pairs={{0,1},{1,0},{2,3},{3,2},{4,5},{5,4},{6,7},{7,6}} | collective-permute-start | bytes 4718600 | tf_op jit(solution)/shard_map/ppermute | solution.py:533
  2169.9 135.4 %collective-permute-start.176 = (bf16[3072,256]{1,0:T(8,128)(2,1)S(1)}, bf16[3072,256]{1,0:T(8,128)(2,1)S(1)}, u32[]{:S(2)}, u32[]{:S(2)}) collective-permute-start(bf16[3072,256]{1,0:T(8,128)(2,1)S(1)} %collective-permute-done.175.refs_0_), channel_id=1, source_target_pairs={{0,4},{2,6},{4,0},{6,2},{1,5},{3,7},{5,1},{7,3}} | collective-permute-start | bytes 4718600 | tf_op jit(solution)/shard_map/ppermute | solution.py:531
  2190.9 89.1 %collective-permute-start.128 = (bf16[768,768]{1,0:T(8,128)(2,1)}, bf16[768,768]{1,0:T(8,128)(2,1)S(1)}, u32[]{:S(2)}, u32[]{:S(2)}) collective-permute-start(bf16[768,768]{1,0:T(8,128)(2,1)} %collective-permute-done.127.refs_0_), channel_id=1, source_target_pairs={{0,4},{2,6},{4,0},{6,2},{1,5},{3,7},{5,1},{7,3}} | collective-permute-start | bytes 3538952 | tf_op jit(solution)/shard_map/ppermute | solution.py:531
  2192.1 113.2 %collective-permute-start.151 = (bf16[768,768]{1,0:T(8,128)(2,1)S(1)}, bf16[768,768]{1,0:T(8,128)(2,1)S(1)}, u32[]{:S(2)}, u32[]{:S(2)}) collective-permute-start(bf16[768,768]{1,0:T(8,128)(2,1)S(1)} %collective-permute-done.150.refs_0_), channel_id=1, source_target_pairs={{0,4},{2,6},{4,0},{6,2},{1,5},{3,7},{5,1},{7,3}} | collective-permute-start | bytes 3538952 | tf_op jit(solution)/shard_map/ppermute | solution.py:531
  2195.7 162.8 %collective-permute-start.170 = (bf16[768,768]{1,0:T(8,128)(2,1)}, bf16[768,768]{1,0:T(8,128)(2,1)}, u32[]{:S(2)}, u32[]{:S(2)}) collective-permute-start(bf16[768,768]{1,0:T(8,128)(2,1)} %collective-permute-done.169.refs_0_), channel_id=1, source_target_pairs={{0,4},{2,6},{4,0},{6,2},{1,5},{3,7},{5,1},{7,3}} | collective-permute-start | bytes 3538952 | tf_op jit(solution)/shard_map/ppermute | solution.py:531
  2254.7 107.8 %collective-permute-start.165 = (bf16[768,768]{1,0:T(8,128)(2,1)}, bf16[768,768]{1,0:T(8,128)(2,1)}, u32[]{:S(2)}, u32[]{:S(2)}) collective-permute-start(bf16[768,768]{1,0:T(8,128)(2,1)} %get-tuple-element.472), channel_id=1, source_target_pairs={{0,1},{1,0},{2,3},{3,2},{4,5},{5,4},{6,7},{7,6}} | collective-permute-start | bytes 3538952 | tf_op jit(solution)/shard_map/ppermute | solution.py:533
  2280.0 82.6 %collective-permute-start.167 = (bf16[768,768]{1,0:T(8,128)(2,1)}, bf16[768,768]{1,0:T(8,128)(2,1)}, u32[]{:S(2)}, u32[]{:S(2)}) collective-permute-start(bf16[768,768]{1,0:T(8,128)(2,1)} %copy-done.13), channel_id=1, source_target_pairs={{0,4},{2,6},{4,0},{6,2},{1,5},{3,7},{5,1},{7,3}} | collective-permute-start | bytes 3538952 | tf_op jit(solution)/shard_map/ppermute | solution.py:531
  (242 other events, 10812.0 us)
